TPU v7x, 8 devices: a whole 2x2x1 slice. The times are simulated.
8 devices in a mesh: heads: 1 (over z), cpo: 2 (over y), cp: 4 (over x, core).
Axes of the slice: x: 2, y: 2, z: 1, core: 2. Of those that a mesh axis runs over, the one named last changes fastest.
Arguments:
- queries: bfloat16 [24, 64, 128, 128], P(None, ('cpo', 'cp'), 'heads')
- attn_out: bfloat16 [24, 64, 128, 128], P(None, ('cpo', 'cp'), 'heads')
- grad_out: bfloat16 [24, 64, 128, 128], P(None, ('cpo', 'cp'), 'heads')
- log_sum_exp: float32 [24, 64, 128], P(None, ('cpo', 'cp'), 'heads')
- key_cache: bfloat16 [9728, 8, 128], P(('cpo', 'cp'), 'heads')
- value_cache: bfloat16 [9728, 8, 128], P(('cpo', 'cp'), 'heads')
Outputs:
- output 1: bfloat16 [24, 64, 128, 128], P(None, ('cpo', 'cp'), 'heads')
- output 2: float32 [9728, 8, 128], P(('cpo', 'cp'), 'heads')
- output 3: float32 [9728, 8, 128], P(('cpo', 'cp'), 'heads')
All inputs are finite; a program needn't handle non-finite values.
Results may differ from a plain program's by a relative error of at most 0.001.
Values are sent between devices in bfloat16 or wider.
A program may use at most 1 GiB of HBM per device.

v0:
```python
import jax
import jax.numpy as jnp
from jax import lax
from jax.sharding import PartitionSpec as P

CP_AXES = ('cpo', 'cp')


def rows_per_step(n_rows, row_width):
    block_rows = n_rows
    while block_rows % 2 == 0 and block_rows * row_width > 4194304:
        block_rows = block_rows // 2
    return block_rows


def make_step(key_part, value_part, key_pos, softmax_scale):
    def block_step(carry_acc, operand):
        acc_key, acc_value = carry_acc
        q_blk, g_blk, stat_blk, row_start = operand
        lse_rows = jnp.transpose(stat_blk[..., 0], (1, 0, 2))
        delta_rows = jnp.transpose(stat_blk[..., 1], (1, 0, 2))
        scores = jnp.einsum('rhgd,khd->hrgk', q_blk, key_part, preferred_element_type=jnp.float32)
        q_pos = row_start + jnp.arange(q_blk.shape[0])
        visible = (key_pos[None, :] <= q_pos[:, None])[None, :, None, :]
        attn_prob = jnp.where(visible, jnp.exp(scores * softmax_scale - lse_rows[..., None]), 0.0)
        acc_value = acc_value + jnp.einsum('hrgk,rhgd->hkd', attn_prob.astype(jnp.bfloat16), g_blk, preferred_element_type=jnp.float32)
        grad_prob = jnp.einsum('rhgd,khd->hrgk', g_blk, value_part, preferred_element_type=jnp.float32)
        grad_scores = (attn_prob * (grad_prob - delta_rows[..., None])).astype(jnp.bfloat16)
        dq_blk = jnp.einsum('hrgk,khd->rhgd', grad_scores, key_part, preferred_element_type=jnp.float32) * softmax_scale
        acc_key = acc_key + softmax_scale * jnp.einsum('hrgk,rhgd->hkd', grad_scores, q_blk, preferred_element_type=jnp.float32)
        return (acc_key, acc_value), dq_blk

    return block_step


def solution(mesh):
    n_dev = mesh.shape['cpo'] * mesh.shape['cp']
    inner_size = mesh.shape['cp']
    row_spec = P(None, CP_AXES, 'heads', None)
    stat_spec = P(None, CP_AXES, 'heads')
    key_spec = P(CP_AXES, 'heads', None)

    def local_grads(queries, attn_out, grad_out, log_sum_exp, key_cache, value_cache):
        n_slices, rows_dev, q_heads, head_dim = queries.shape
        key_rows = key_cache.shape[0]
        kv_heads = key_cache.shape[1]
        group_size = q_heads // kv_heads
        slice_len = rows_dev * n_dev
        prefix_base = key_rows * n_dev - n_slices * slice_len
        softmax_scale = head_dim ** -0.5
        dev_idx = lax.axis_index('cpo') * inner_size + lax.axis_index('cp')
        key_pos = dev_idx * key_rows + jnp.arange(key_rows)
        block_rows = rows_per_step(slice_len, q_heads * key_rows)
        n_blocks = slice_len // block_rows
        blk_shape = (n_blocks, block_rows, kv_heads, group_size)
        row_delta = jnp.sum(grad_out.astype(jnp.float32) * attn_out.astype(jnp.float32), axis=-1)
        row_stats = jnp.stack([log_sum_exp, row_delta], axis=-1)
        block_step = make_step(key_cache, value_cache, key_pos, softmax_scale)
        acc_key = jnp.zeros((kv_heads, key_rows, head_dim), jnp.float32)
        acc_value = jnp.zeros((kv_heads, key_rows, head_dim), jnp.float32)
        dq_list = []
        for slice_idx in reversed(range(n_slices)):
            q_all = lax.all_gather(queries[slice_idx], CP_AXES, axis=0, tiled=True)
            g_all = lax.all_gather(grad_out[slice_idx], CP_AXES, axis=0, tiled=True)
            stat_all = lax.all_gather(row_stats[slice_idx], CP_AXES, axis=0, tiled=True)
            row_starts = prefix_base + slice_idx * slice_len + block_rows * jnp.arange(n_blocks)
            operands = (q_all.reshape(blk_shape + (head_dim,)), g_all.reshape(blk_shape + (head_dim,)), stat_all.reshape(blk_shape + (2,)), row_starts)
            (acc_key, acc_value), dq_blocks = lax.scan(block_step, (acc_key, acc_value), operands)
            dq_part = dq_blocks.reshape(slice_len, q_heads, head_dim)
            dq_list.append(lax.psum_scatter(dq_part, CP_AXES, scatter_dimension=0, tiled=True).astype(jnp.bfloat16))
        grad_query = jnp.stack(dq_list[::-1])
        return grad_query, jnp.transpose(acc_key, (1, 0, 2)), jnp.transpose(acc_value, (1, 0, 2))

    return jax.shard_map(local_grads, mesh=mesh, in_specs=(row_spec, row_spec, row_spec, stat_spec, key_spec, key_spec), out_specs=(row_spec, key_spec, key_spec), check_vma=False)
```

profile of v0, /device:TPU:0, one launch (start us, length us, event | category | flops | bytes accessed | tf_op | source)
XLA Modules:
  0.0 5064.8 jit_solution(14496071535695691402)
XLA Ops:
  71.3 14.1 all-gather.1
  375.2 131.1 %while.383 = (s32[]{:T(128)}, f32[8,1216,128]{2,1,0:T(8,128)}, f32[8,1216,128]{2,1,0:T(8,128)}, f32[4,16,8,16,128]{4,3,2,1,0:T(8,128)}, s32[4]{0:T(128)S(1)}, /*...) while((s32[]{:T(128)}, f32[8,1216,128]{2,1,0:T(8,128)}, ...), condition=%wide.region_2.3_spmd.clone, body=%wide.region_1.2_spmd.clone.sunk | while | flops 3219083520 | bytes 145509392 | solution.py:68
  508.9 147.8 %while.360 = (s32[]{:T(128)}, f32[8,1216,128]{2,1,0:T(8,128)}, f32[8,1216,128]{2,1,0:T(8,128)}, f32[4,16,8,16,128]{4,3,2,1,0:T(8,128)}, s32[4]{0:T(128)S(1)}, /*...) while((s32[]{:T(128)}, f32[8,1216,128]{2,1,0:T(8,128)}, ...), condition=%wide.region_4.5_spmd.clone, body=%wide.region_3.4_spmd.clone.sunk | while | flops 3216593152 | bytes 164424624 | solution.py:68
  565.5 12.5 bitcast_add_fusion.48
  659.3 147.6 %while.361 = (s32[]{:T(128)}, f32[8,1216,128]{2,1,0:T(8,128)}, f32[8,1216,128]{2,1,0:T(8,128)}, f32[4,16,8,16,128]{4,3,2,1,0:T(8,128)}, s32[4]{0:T(128)S(1)}, /*...) while((s32[]{:T(128)}, f32[8,1216,128]{2,1,0:T(8,128)}, ...), condition=%wide.region_6.7_spmd.clone, body=%wide.region_5.6_spmd.clone.sunk | while | flops 3216593152 | bytes 164424624 | solution.py:68
  715.6 12.5 bitcast_add_fusion.49
  809.4 147.8 %while.362 = (s32[]{:T(128)}, f32[8,1216,128]{2,1,0:T(8,128)}, f32[8,1216,128]{2,1,0:T(8,128)}, f32[4,16,8,16,128]{4,3,2,1,0:T(8,128)}, s32[4]{0:T(128)S(1)}, /*...) while((s32[]{:T(128)}, f32[8,1216,128]{2,1,0:T(8,128)}, ...), condition=%wide.region_8.9_spmd.clone, body=%wide.region_7.8_spmd.clone.sunk | while | flops 3216593152 | bytes 164424624 | solution.py:68
  829.0 12.5 bitcast_add_fusion.50
  902.8 12.5 bitcast_add_fusion.50
  939.6 12.5 bitcast_add_fusion.50
  959.7 147.6 %while.363 = (s32[]{:T(128)}, f32[8,1216,128]{2,1,0:T(8,128)}, f32[8,1216,128]{2,1,0:T(8,128)}, f32[4,16,8,16,128]{4,3,2,1,0:T(8,128)}, s32[4]{0:T(128)S(1)}, /*...) while((s32[]{:T(128)}, f32[8,1216,128]{2,1,0:T(8,128)}, ...), condition=%wide.region_10.11_spmd.clone, body=%wide.region_9.10_spmd.clone.sunk | while | flops 3216593152 | bytes 164424624 | solution.py:68
  979.1 12.5 bitcast_add_fusion.51
  1089.7 12.5 bitcast_add_fusion.51
  1109.9 147.8 %while.364 = (s32[]{:T(128)}, f32[8,1216,128]{2,1,0:T(8,128)}, f32[8,1216,128]{2,1,0:T(8,128)}, f32[4,16,8,16,128]{4,3,2,1,0:T(8,128)}, s32[4]{0:T(128)S(1)}, /*...) while((s32[]{:T(128)}, f32[8,1216,128]{2,1,0:T(8,128)}, ...), condition=%wide.region_12.13_spmd.clone, body=%wide.region_11.12_spmd.clone.sunk | while | flops 3216593152 | bytes 164424624 | solution.py:68
  1166.5 12.5 bitcast_add_fusion.52
  1203.3 12.5 bitcast_add_fusion.52
  1260.2 147.6 %while.365 = (s32[]{:T(128)}, f32[8,1216,128]{2,1,0:T(8,128)}, f32[8,1216,128]{2,1,0:T(8,128)}, f32[4,16,8,16,128]{4,3,2,1,0:T(8,128)}, s32[4]{0:T(128)S(1)}, /*...) while((s32[]{:T(128)}, f32[8,1216,128]{2,1,0:T(8,128)}, ...), condition=%wide.region_14.15_spmd.clone, body=%wide.region_13.14_spmd.clone.sunk | while | flops 3216593152 | bytes 164424624 | solution.py:68
  1316.6 12.5 bitcast_add_fusion.53
  1390.3 12.5 bitcast_add_fusion.53
  1410.3 147.8 %while.366 = (s32[]{:T(128)}, f32[8,1216,128]{2,1,0:T(8,128)}, f32[8,1216,128]{2,1,0:T(8,128)}, f32[4,16,8,16,128]{4,3,2,1,0:T(8,128)}, s32[4]{0:T(128)S(1)}, /*...) while((s32[]{:T(128)}, f32[8,1216,128]{2,1,0:T(8,128)}, ...), condition=%wide.region_16.17_spmd.clone, body=%wide.region_15.16_spmd.clone.sunk | while | flops 3216593152 | bytes 164424624 | solution.py:68
  1430.0 12.5 bitcast_add_fusion.54
  1503.7 12.5 bitcast_add_fusion.54
  1540.6 12.5 bitcast_add_fusion.54
  1560.6 147.6 %while.367 = (s32[]{:T(128)}, f32[8,1216,128]{2,1,0:T(8,128)}, f32[8,1216,128]{2,1,0:T(8,128)}, f32[4,16,8,16,128]{4,3,2,1,0:T(8,128)}, s32[4]{0:T(128)S(1)}, /*...) while((s32[]{:T(128)}, f32[8,1216,128]{2,1,0:T(8,128)}, ...), condition=%wide.region_18.19_spmd.clone, body=%wide.region_17.18_spmd.clone.sunk | while | flops 3216593152 | bytes 164424624 | solution.py:68
  1617.0 12.5 bitcast_add_fusion.55
  1710.9 147.8 %while.368 = (s32[]{:T(128)}, f32[8,1216,128]{2,1,0:T(8,128)}, f32[8,1216,128]{2,1,0:T(8,128)}, f32[4,16,8,16,128]{4,3,2,1,0:T(8,128)}, s32[4]{0:T(128)S(1)}, /*...) while((s32[]{:T(128)}, f32[8,1216,128]{2,1,0:T(8,128)}, ...), condition=%wide.region_20.21_spmd.clone, body=%wide.region_19.20_spmd.clone.sunk | while | flops 3216593152 | bytes 164424624 | solution.py:68
  1861.2 147.6 %while.369 = (s32[]{:T(128)}, f32[8,1216,128]{2,1,0:T(8,128)}, f32[8,1216,128]{2,1,0:T(8,128)}, f32[4,16,8,16,128]{4,3,2,1,0:T(8,128)}, s32[4]{0:T(128)S(1)}, /*...) while((s32[]{:T(128)}, f32[8,1216,128]{2,1,0:T(8,128)}, ...), condition=%wide.region_22.23_spmd.clone, body=%wide.region_21.22_spmd.clone.sunk | while | flops 3216593152 | bytes 164424624 | solution.py:68
  2011.4 147.8 %while.370 = (s32[]{:T(128)}, f32[8,1216,128]{2,1,0:T(8,128)}, f32[8,1216,128]{2,1,0:T(8,128)}, f32[4,16,8,16,128]{4,3,2,1,0:T(8,128)}, s32[4]{0:T(128)S(1)}, /*...) while((s32[]{:T(128)}, f32[8,1216,128]{2,1,0:T(8,128)}, ...), condition=%wide.region_24.25_spmd.clone, body=%wide.region_23.24_spmd.clone.sunk | while | flops 3216593152 | bytes 164424624 | solution.py:68
  2161.8 147.6 %while.371 = (s32[]{:T(128)}, f32[8,1216,128]{2,1,0:T(8,128)}, f32[8,1216,128]{2,1,0:T(8,128)}, f32[4,16,8,16,128]{4,3,2,1,0:T(8,128)}, s32[4]{0:T(128)S(1)}, /*...) while((s32[]{:T(128)}, f32[8,1216,128]{2,1,0:T(8,128)}, ...), condition=%wide.region_26.27_spmd.clone, body=%wide.region_25.26_spmd.clone.sunk | while | flops 3216593152 | bytes 164424624 | solution.py:68
  2312.1 147.9 %while.372 = (s32[]{:T(128)}, f32[8,1216,128]{2,1,0:T(8,128)}, f32[8,1216,128]{2,1,0:T(8,128)}, f32[4,16,8,16,128]{4,3,2,1,0:T(8,128)}, s32[4]{0:T(128)S(1)}, /*...) while((s32[]{:T(128)}, f32[8,1216,128]{2,1,0:T(8,128)}, ...), condition=%wide.region_28.29_spmd.clone, body=%wide.region_27.28_spmd.clone.sunk | while | flops 3216593152 | bytes 164424624 | solution.py:68
  2462.5 147.6 %while.373 = (s32[]{:T(128)}, f32[8,1216,128]{2,1,0:T(8,128)}, f32[8,1216,128]{2,1,0:T(8,128)}, f32[4,16,8,16,128]{4,3,2,1,0:T(8,128)}, s32[4]{0:T(128)S(1)}, /*...) while((s32[]{:T(128)}, f32[8,1216,128]{2,1,0:T(8,128)}, ...), condition=%wide.region_30.31_spmd.clone, body=%wide.region_29.30_spmd.clone.sunk | while | flops 3216593152 | bytes 164424624 | solution.py:68
  2612.6 147.9 %while.374 = (s32[]{:T(128)}, f32[8,1216,128]{2,1,0:T(8,128)}, f32[8,1216,128]{2,1,0:T(8,128)}, f32[4,16,8,16,128]{4,3,2,1,0:T(8,128)}, s32[4]{0:T(128)S(1)}, /*...) while((s32[]{:T(128)}, f32[8,1216,128]{2,1,0:T(8,128)}, ...), condition=%wide.region_32.33_spmd.clone, body=%wide.region_31.32_spmd.clone.sunk | while | flops 3216593152 | bytes 164424624 | solution.py:68
  2763.0 147.6 %while.375 = (s32[]{:T(128)}, f32[8,1216,128]{2,1,0:T(8,128)}, f32[8,1216,128]{2,1,0:T(8,128)}, f32[4,16,8,16,128]{4,3,2,1,0:T(8,128)}, s32[4]{0:T(128)S(1)}, /*...) while((s32[]{:T(128)}, f32[8,1216,128]{2,1,0:T(8,128)}, ...), condition=%wide.region_34.35_spmd.clone, body=%wide.region_33.34_spmd.clone.sunk | while | flops 3216593152 | bytes 164424624 | solution.py:68
  2913.3 147.9 %while.376 = (s32[]{:T(128)}, f32[8,1216,128]{2,1,0:T(8,128)}, f32[8,1216,128]{2,1,0:T(8,128)}, f32[4,16,8,16,128]{4,3,2,1,0:T(8,128)}, s32[4]{0:T(128)S(1)}, /*...) while((s32[]{:T(128)}, f32[8,1216,128]{2,1,0:T(8,128)}, ...), condition=%wide.region_36.37_spmd.clone, body=%wide.region_35.36_spmd.clone.sunk | while | flops 3216593152 | bytes 164424624 | solution.py:68
  3063.7 147.6 %while.377 = (s32[]{:T(128)}, f32[8,1216,128]{2,1,0:T(8,128)}, f32[8,1216,128]{2,1,0:T(8,128)}, f32[4,16,8,16,128]{4,3,2,1,0:T(8,128)}, s32[4]{0:T(128)S(1)}, /*...) while((s32[]{:T(128)}, f32[8,1216,128]{2,1,0:T(8,128)}, ...), condition=%wide.region_38.39_spmd.clone, body=%wide.region_37.38_spmd.clone.sunk | while | flops 3216593152 | bytes 164424624 | solution.py:68
  3213.7 147.8 %while.378 = (s32[]{:T(128)}, f32[8,1216,128]{2,1,0:T(8,128)}, f32[8,1216,128]{2,1,0:T(8,128)}, f32[4,16,8,16,128]{4,3,2,1,0:T(8,128)}, s32[4]{0:T(128)S(1)}, /*...) while((s32[]{:T(128)}, f32[8,1216,128]{2,1,0:T(8,128)}, ...), condition=%wide.region_40.41_spmd.clone, body=%wide.region_39.40_spmd.clone.sunk | while | flops 3216593152 | bytes 164424624 | solution.py:68
  3364.1 147.6 %while.379 = (s32[]{:T(128)}, f32[8,1216,128]{2,1,0:T(8,128)}, f32[8,1216,128]{2,1,0:T(8,128)}, f32[4,16,8,16,128]{4,3,2,1,0:T(8,128)}, s32[4]{0:T(128)S(1)}, /*...) while((s32[]{:T(128)}, f32[8,1216,128]{2,1,0:T(8,128)}, ...), condition=%wide.region_42.43_spmd.clone, body=%wide.region_41.42_spmd.clone.sunk | while | flops 3216593152 | bytes 164424624 | solution.py:68
  3514.3 147.9 %while.380 = (s32[]{:T(128)}, f32[8,1216,128]{2,1,0:T(8,128)}, f32[8,1216,128]{2,1,0:T(8,128)}, f32[4,16,8,16,128]{4,3,2,1,0:T(8,128)}, s32[4]{0:T(128)S(1)}, /*...) while((s32[]{:T(128)}, f32[8,1216,128]{2,1,0:T(8,128)}, ...), condition=%wide.region_44.45_spmd.clone, body=%wide.region_43.44_spmd.clone.sunk | while | flops 3216593152 | bytes 164424624 | solution.py:68
  3664.6 147.6 %while.381 = (s32[]{:T(128)}, f32[8,1216,128]{2,1,0:T(8,128)}, f32[8,1216,128]{2,1,0:T(8,128)}, f32[4,16,8,16,128]{4,3,2,1,0:T(8,128)}, s32[4]{0:T(128)S(1)}, /*...) while((s32[]{:T(128)}, f32[8,1216,128]{2,1,0:T(8,128)}, ...), condition=%wide.region_46.47_spmd.clone, body=%wide.region_45.46_spmd.clone.sunk | while | flops 3216593152 | bytes 164424624 | solution.py:68
  3814.7 147.7 %while.382 = (s32[]{:T(128)}, f32[8,1216,128]{2,1,0:T(8,128)}, f32[8,1216,128]{2,1,0:T(8,128)}, f32[4,16,8,16,128]{4,3,2,1,0:T(8,128)}, s32[4]{0:T(128)S(1)}, /*...) while((s32[]{:T(128)}, f32[8,1216,128]{2,1,0:T(8,128)}, ...), condition=%wide.region_48.49_spmd.clone, body=%wide.region_47.48_spmd.clone.sunk | while | flops 3216593152 | bytes 164424624 | solution.py:68
  3977.8 16.3 copy_bitcast_fusion.168
  4006.8 44.0 reduce-scatter.27.cloned.1.call-done
  4052.6 43.9 reduce-scatter.29.cloned.1.call-done
  4098.2 44.0 reduce-scatter.31.cloned.1.call-done
  4144.0 43.8 reduce-scatter.33.cloned.1.call-done
  4189.6 44.0 reduce-scatter.35.cloned.1.call-done
  4235.4 44.0 reduce-scatter.37.cloned.1.call-done
  4281.2 43.9 reduce-scatter.39.cloned.1.call-done
  4326.9 44.0 reduce-scatter.41.cloned.1.call-done
  4372.7 43.8 reduce-scatter.43.cloned.1.call-done
  4418.3 43.8 reduce-scatter.45.cloned.1.call-done
  4463.9 44.0 reduce-scatter.47.cloned.1.call-done
  4509.6 44.0 reduce-scatter.49.cloned.1.call-done
  4555.4 44.0 reduce-scatter.51.cloned.1.call-done
  4601.2 43.8 reduce-scatter.53.cloned.1.call-done
  4646.8 43.8 reduce-scatter.55.cloned.1.call-done
  4692.4 44.0 reduce-scatter.57.cloned.1.call-done
  4738.1 43.8 reduce-scatter.59.cloned.1.call-done
  4783.7 43.8 reduce-scatter.61.cloned.1.call-done
  4829.4 44.0 reduce-scatter.63.cloned.1.call-done
  4875.1 44.0 reduce-scatter.65.cloned.1.call-done
  4920.9 43.8 reduce-scatter.67.cloned.1.call-done
  4966.5 44.0 reduce-scatter.69.cloned.1.call-done
  5012.2 43.8 reduce-scatter.71.cloned.1.call-done
  (2783 shorter events, 3804.2 us)
Async XLA Ops:
  7.2 365.5 %all-gather.121.cloned.1.call-start = ((), (), s32[]{:S(2)}) async-start(), calls=%async_computation.48 | async-start | bytes 2359296 | tf_op jit(solution)/shard_map/all_gather | solution.py:63
  12.0 494.3 %all-gather.125.cloned.1.call-start = ((), (), s32[]{:S(2)}) async-start(), calls=%async_computation.50 | async-start | bytes 2359296 | tf_op jit(solution)/shard_map/all_gather | solution.py:63
  12.7 493.6 %all-gather.127.cloned.1.call-start = ((), (), s32[]{:S(2)}) async-start(), calls=%async_computation.51 | async-start | bytes 2359296 | tf_op jit(solution)/shard_map/all_gather | solution.py:64
  13.3 643.5 %all-gather.129.cloned.1.call-start = ((), (), s32[]{:S(2)}) async-start(), calls=%async_computation.52 | async-start | bytes 2359296 | tf_op jit(solution)/shard_map/all_gather | solution.py:63
  13.9 642.9 %all-gather.131.cloned.1.call-start = ((), (), s32[]{:S(2)}) async-start(), calls=%async_computation.53 | async-start | bytes 2359296 | tf_op jit(solution)/shard_map/all_gather | solution.py:64
  14.5 792.4 %all-gather.133.cloned.1.call-start = ((), (), s32[]{:S(2)}) async-start(), calls=%async_computation.54 | async-start | bytes 2359296 | tf_op jit(solution)/shard_map/all_gather | solution.py:63
  15.2 791.7 %all-gather.135.cloned.1.call-start = ((), (), s32[]{:S(2)}) async-start(), calls=%async_computation.55 | async-start | bytes 2359296 | tf_op jit(solution)/shard_map/all_gather | solution.py:64
  16.0 941.2 %all-gather.137.cloned.1.call-start = ((), (), s32[]{:S(2)}) async-start(), calls=%async_computation.56 | async-start | bytes 2359296 | tf_op jit(solution)/shard_map/all_gather | solution.py:63
  16.7 940.5 %all-gather.139.cloned.1.call-start = ((), (), s32[]{:S(2)}) async-start(), calls=%async_computation.57 | async-start | bytes 2359296 | tf_op jit(solution)/shard_map/all_gather | solution.py:64
  17.3 1090.0 %all-gather.141.cloned.1.call-start = ((), (), s32[]{:S(2)}) async-start(), calls=%async_computation.58 | async-start | bytes 2359296 | tf_op jit(solution)/shard_map/all_gather | solution.py:63
  22.0 1085.3 %all-gather.143.cloned.1.call-start = ((), (), s32[]{:S(2)}) async-start(), calls=%async_computation.59 | async-start | bytes 2359296 | tf_op jit(solution)/shard_map/all_gather | solution.py:64
  26.7 1231.0 %all-gather.145.cloned.1.call-start = ((), (), s32[]{:S(2)}) async-start(), calls=%async_computation.60 | async-start | bytes 2359296 | tf_op jit(solution)/shard_map/all_gather | solution.py:63
  27.5 1230.3 %all-gather.147.cloned.1.call-start = ((), (), s32[]{:S(2)}) async-start(), calls=%async_computation.61 | async-start | bytes 2359296 | tf_op jit(solution)/shard_map/all_gather | solution.py:64
  28.0 1379.8 %all-gather.149.cloned.1.call-start = ((), (), s32[]{:S(2)}) async-start(), calls=%async_computation.62 | async-start | bytes 2359296 | tf_op jit(solution)/shard_map/all_gather | solution.py:63
  28.6 1379.2 %all-gather.151.cloned.1.call-start = ((), (), s32[]{:S(2)}) async-start(), calls=%async_computation.63 | async-start | bytes 2359296 | tf_op jit(solution)/shard_map/all_gather | solution.py:64
  29.2 1528.9 %all-gather.153.cloned.1.call-start = ((), (), s32[]{:S(2)}) async-start(), calls=%async_computation.64 | async-start | bytes 2359296 | tf_op jit(solution)/shard_map/all_gather | solution.py:63
  29.8 1528.4 %all-gather.155.cloned.1.call-start = ((), (), s32[]{:S(2)}) async-start(), calls=%async_computation.65 | async-start | bytes 2359296 | tf_op jit(solution)/shard_map/all_gather | solution.py:64
  30.4 1677.9 %all-gather.157.cloned.1.call-start = ((), (), s32[]{:S(2)}) async-start(), calls=%async_computation.66 | async-start | bytes 2359296 | tf_op jit(solution)/shard_map/all_gather | solution.py:63
  31.1 1677.2 %all-gather.159.cloned.1.call-start = ((), (), s32[]{:S(2)}) async-start(), calls=%async_computation.67 | async-start | bytes 2359296 | tf_op jit(solution)/shard_map/all_gather | solution.py:64
  31.7 1827.0 %all-gather.161.cloned.1.call-start = ((), (), s32[]{:S(2)}) async-start(), calls=%async_computation.68 | async-start | bytes 2359296 | tf_op jit(solution)/shard_map/all_gather | solution.py:63
  32.4 1826.3 %all-gather.163.cloned.1.call-start = ((), (), s32[]{:S(2)}) async-start(), calls=%async_computation.69 | async-start | bytes 2359296 | tf_op jit(solution)/shard_map/all_gather | solution.py:64
  33.2 1975.7 %all-gather.165.cloned.1.call-start = ((), (), s32[]{:S(2)}) async-start(), calls=%async_computation.70 | async-start | bytes 2359296 | tf_op jit(solution)/shard_map/all_gather | solution.py:63
  33.9 1974.9 %all-gather.167.cloned.1.call-start = ((), (), s32[]{:S(2)}) async-start(), calls=%async_computation.71 | async-start | bytes 2359296 | tf_op jit(solution)/shard_map/all_gather | solution.py:64
  34.5 2124.8 %all-gather.169.cloned.1.call-start = ((), (), s32[]{:S(2)}) async-start(), calls=%async_computation.72 | async-start | bytes 2359296 | tf_op jit(solution)/shard_map/all_gather | solution.py:63
  35.2 2124.0 %all-gather.171.cloned.1.call-start = ((), (), s32[]{:S(2)}) async-start(), calls=%async_computation.73 | async-start | bytes 2359296 | tf_op jit(solution)/shard_map/all_gather | solution.py:64
  35.8 2273.6 %all-gather.173.cloned.1.call-start = ((), (), s32[]{:S(2)}) async-start(), calls=%async_computation.74 | async-start | bytes 2359296 | tf_op jit(solution)/shard_map/all_gather | solution.py:63
  36.4 2273.0 %all-gather.175.cloned.1.call-start = ((), (), s32[]{:S(2)}) async-start(), calls=%async_computation.75 | async-start | bytes 2359296 | tf_op jit(solution)/shard_map/all_gather | solution.py:64
  37.2 2422.8 %all-gather.177.cloned.1.call-start = ((), (), s32[]{:S(2)}) async-start(), calls=%async_computation.76 | async-start | bytes 2359296 | tf_op jit(solution)/shard_map/all_gather | solution.py:63
  37.9 2422.1 %all-gather.179.cloned.1.call-start = ((), (), s32[]{:S(2)}) async-start(), calls=%async_computation.77 | async-start | bytes 2359296 | tf_op jit(solution)/shard_map/all_gather | solution.py:64
  38.5 2571.6 %all-gather.181.cloned.1.call-start = ((), (), s32[]{:S(2)}) async-start(), calls=%async_computation.78 | async-start | bytes 2359296 | tf_op jit(solution)/shard_map/all_gather | solution.py:63
  39.2 2570.8 %all-gather.183.cloned.1.call-start = ((), (), s32[]{:S(2)}) async-start(), calls=%async_computation.79 | async-start | bytes 2359296 | tf_op jit(solution)/shard_map/all_gather | solution.py:64
  40.0 2720.6 %all-gather.185.cloned.1.call-start = ((), (), s32[]{:S(2)}) async-start(), calls=%async_computation.80 | async-start | bytes 2359296 | tf_op jit(solution)/shard_map/all_gather | solution.py:63
  40.5 2720.0 %all-gather.187.cloned.1.call-start = ((), (), s32[]{:S(2)}) async-start(), calls=%async_computation.81 | async-start | bytes 2359296 | tf_op jit(solution)/shard_map/all_gather | solution.py:64
  41.3 2869.4 %all-gather.189.cloned.1.call-start = ((), (), s32[]{:S(2)}) async-start(), calls=%async_computation.82 | async-start | bytes 2359296 | tf_op jit(solution)/shard_map/all_gather | solution.py:63
  42.0 2868.6 %all-gather.191.cloned.1.call-start = ((), (), s32[]{:S(2)}) async-start(), calls=%async_computation.83 | async-start | bytes 2359296 | tf_op jit(solution)/shard_map/all_gather | solution.py:64
  42.6 3018.6 %all-gather.193.cloned.1.call-start = ((), (), s32[]{:S(2)}) async-start(), calls=%async_computation.84 | async-start | bytes 2359296 | tf_op jit(solution)/shard_map/all_gather | solution.py:63
  43.2 3018.0 %all-gather.195.cloned.1.call-start = ((), (), s32[]{:S(2)}) async-start(), calls=%async_computation.85 | async-start | bytes 2359296 | tf_op jit(solution)/shard_map/all_gather | solution.py:64
  43.9 3167.3 %all-gather.197.cloned.1.call-start = ((), (), s32[]{:S(2)}) async-start(), calls=%async_computation.86 | async-start | bytes 2359296 | tf_op jit(solution)/shard_map/all_gather | solution.py:63
  44.5 3166.7 %all-gather.199.cloned.1.call-start = ((), (), s32[]{:S(2)}) async-start(), calls=%async_computation.87 | async-start | bytes 2359296 | tf_op jit(solution)/shard_map/all_gather | solution.py:64
  45.2 3316.3 %all-gather.201.cloned.1.call-start = ((), (), s32[]{:S(2)}) async-start(), calls=%async_computation.88 | async-start | bytes 2359296 | tf_op jit(solution)/shard_map/all_gather | solution.py:63
  46.0 3315.6 %all-gather.203.cloned.1.call-start = ((), (), s32[]{:S(2)}) async-start(), calls=%async_computation.89 | async-start | bytes 2359296 | tf_op jit(solution)/shard_map/all_gather | solution.py:64
  46.7 3465.0 %all-gather.205.cloned.1.call-start = ((), (), s32[]{:S(2)}) async-start(), calls=%async_computation.90 | async-start | bytes 2359296 | tf_op jit(solution)/shard_map/all_gather | solution.py:63
  47.3 3464.4 %all-gather.207.cloned.1.call-start = ((), (), s32[]{:S(2)}) async-start(), calls=%async_computation.91 | async-start | bytes 2359296 | tf_op jit(solution)/shard_map/all_gather | solution.py:64
  48.1 3614.1 %all-gather.209.cloned.1.call-start = ((), (), s32[]{:S(2)}) async-start(), calls=%async_computation.92 | async-start | bytes 2359296 | tf_op jit(solution)/shard_map/all_gather | solution.py:63
  48.6 3613.6 %all-gather.211.cloned.1.call-start = ((), (), s32[]{:S(2)}) async-start(), calls=%async_computation.93 | async-start | bytes 2359296 | tf_op jit(solution)/shard_map/all_gather | solution.py:64
  49.2 3763.0 %all-gather.213.cloned.1.call-start = ((), (), s32[]{:S(2)}) async-start(), calls=%async_computation.94 | async-start | bytes 2359296 | tf_op jit(solution)/shard_map/all_gather | solution.py:63
  49.8 3762.4 %all-gather.215.cloned.1.call-start = ((), (), s32[]{:S(2)}) async-start(), calls=%async_computation.95 | async-start | bytes 2359296 | tf_op jit(solution)/shard_map/all_gather | solution.py:64
  50.4 3954.6 %reduce-scatter.25.cloned.1.call-start = ((), (), s32[]{:S(2)}) async-start(), calls=%async_computation.24 | async-start | bytes 4718592 | tf_op jit(solution)/shard_map/reduce_scatter | solution.py:70
  3967.2 403.7 %reduce-scatter.41.cloned.1.call-start = ((), (), s32[]{:S(2)}) async-start(), calls=%async_computation.32 | async-start | bytes 4718592 | tf_op jit(solution)/shard_map/reduce_scatter | solution.py:70
  3968.0 448.5 %reduce-scatter.43.cloned.1.call-start = ((), (), s32[]{:S(2)}) async-start(), calls=%async_computation.33 | async-start | bytes 4718592 | tf_op jit(solution)/shard_map/reduce_scatter | solution.py:70
  3968.6 493.5 %reduce-scatter.45.cloned.1.call-start = ((), (), s32[]{:S(2)}) async-start(), calls=%async_computation.34 | async-start | bytes 4718592 | tf_op jit(solution)/shard_map/reduce_scatter | solution.py:70
  3969.1 538.7 %reduce-scatter.47.cloned.1.call-start = ((), (), s32[]{:S(2)}) async-start(), calls=%async_computation.35 | async-start | bytes 4718592 | tf_op jit(solution)/shard_map/reduce_scatter | solution.py:70
  3969.9 583.7 %reduce-scatter.49.cloned.1.call-start = ((), (), s32[]{:S(2)}) async-start(), calls=%async_computation.36 | async-start | bytes 4718592 | tf_op jit(solution)/shard_map/reduce_scatter | solution.py:70
  3970.6 628.7 %reduce-scatter.51.cloned.1.call-start = ((), (), s32[]{:S(2)}) async-start(), calls=%async_computation.37 | async-start | bytes 4718592 | tf_op jit(solution)/shard_map/reduce_scatter | solution.py:70
  3971.4 673.6 %reduce-scatter.53.cloned.1.call-start = ((), (), s32[]{:S(2)}) async-start(), calls=%async_computation.38 | async-start | bytes 4718592 | tf_op jit(solution)/shard_map/reduce_scatter | solution.py:70
  3972.0 718.6 %reduce-scatter.55.cloned.1.call-start = ((), (), s32[]{:S(2)}) async-start(), calls=%async_computation.39 | async-start | bytes 4718592 | tf_op jit(solution)/shard_map/reduce_scatter | solution.py:70
  3972.5 763.8 %reduce-scatter.57.cloned.1.call-start = ((), (), s32[]{:S(2)}) async-start(), calls=%async_computation.40 | async-start | bytes 4718592 | tf_op jit(solution)/shard_map/reduce_scatter | solution.py:70
  3973.3 808.7 %reduce-scatter.59.cloned.1.call-start = ((), (), s32[]{:S(2)}) async-start(), calls=%async_computation.41 | async-start | bytes 4718592 | tf_op jit(solution)/shard_map/reduce_scatter | solution.py:70
  3973.9 853.7 %reduce-scatter.61.cloned.1.call-start = ((), (), s32[]{:S(2)}) async-start(), calls=%async_computation.42 | async-start | bytes 4718592 | tf_op jit(solution)/shard_map/reduce_scatter | solution.py:70
  3974.4 898.9 %reduce-scatter.63.cloned.1.call-start = ((), (), s32[]{:S(2)}) async-start(), calls=%async_computation.43 | async-start | bytes 4718592 | tf_op jit(solution)/shard_map/reduce_scatter | solution.py:70
  3975.2 943.9 %reduce-scatter.65.cloned.1.call-start = ((), (), s32[]{:S(2)}) async-start(), calls=%async_computation.44 | async-start | bytes 4718592 | tf_op jit(solution)/shard_map/reduce_scatter | solution.py:70
  3975.9 988.8 %reduce-scatter.67.cloned.1.call-start = ((), (), s32[]{:S(2)}) async-start(), calls=%async_computation.45 | async-start | bytes 4718592 | tf_op jit(solution)/shard_map/reduce_scatter | solution.py:70
  3976.5 1033.9 %reduce-scatter.69.cloned.1.call-start = ((), (), s32[]{:S(2)}) async-start(), calls=%async_computation.46 | async-start | bytes 4718592 | tf_op jit(solution)/shard_map/reduce_scatter | solution.py:70
  3977.2 1078.8 %reduce-scatter.71.cloned.1.call-start = ((), (), s32[]{:S(2)}) async-start(), calls=%async_computation.47 | async-start | bytes 4718592 | tf_op jit(solution)/shard_map/reduce_scatter | solution.py:70
  (525 other events, 9173.1 us)
Sparse Core Ops, SparseCore 0:
  10.4 24.7 all-gather.120
  37.0 21.9 all-gather.122
  60.8 22.2 all-gather.124
  84.8 22.2 all-gather.126
  108.8 22.2 all-gather.128
  132.8 22.1 all-gather.130
  156.8 22.1 all-gather.132
  180.8 22.1 all-gather.134
  204.9 22.1 all-gather.136
  228.7 22.1 all-gather.138
  252.8 22.3 all-gather.140
  276.9 22.3 all-gather.142
  301.1 22.5 all-gather.144
  325.4 22.6 all-gather.146
  349.7 22.5 all-gather.148
  397.7 21.9 all-gather.152
  421.3 21.9 all-gather.154
  445.1 21.9 all-gather.156
  468.8 21.9 all-gather.158
  492.6 21.9 all-gather.160
  516.4 21.9 all-gather.162
  540.2 22.0 all-gather.164
  587.7 21.9 all-gather.168
  611.4 21.9 all-gather.170
  635.0 21.9 all-gather.172
  658.8 21.9 all-gather.174
  682.6 21.9 all-gather.176
  706.3 21.9 all-gather.178
  730.1 21.9 all-gather.180
  753.9 21.9 all-gather.182
  777.5 21.9 all-gather.184
  801.4 21.9 all-gather.186
  848.8 21.9 all-gather.190
  872.5 21.9 all-gather.192
  919.9 21.9 all-gather.196
  991.3 21.9 all-gather.202
  1038.8 21.9 all-gather.206
  1086.1 21.9 all-gather.210
  1109.7 21.9 all-gather.212
  1133.4 21.9 all-gather.214
  3962.5 42.4 reduce-scatter.24
  4008.3 42.4 reduce-scatter.26
  4053.9 42.4 reduce-scatter.28
  4099.7 42.4 reduce-scatter.30
  4145.3 42.4 reduce-scatter.32
  4191.1 42.4 reduce-scatter.34
  4236.9 42.4 reduce-scatter.36
  4282.7 42.4 reduce-scatter.38
  4328.4 42.4 reduce-scatter.40
  4374.0 42.3 reduce-scatter.42
  4419.6 42.4 reduce-scatter.44
  4465.4 42.4 reduce-scatter.46
  4511.1 42.4 reduce-scatter.48
  4556.9 42.4 reduce-scatter.50
  4602.5 42.4 reduce-scatter.52
  4648.1 42.4 reduce-scatter.54
  4693.9 42.4 reduce-scatter.56
  4739.5 42.4 reduce-scatter.58
  4785.1 42.4 reduce-scatter.60
  4830.8 42.4 reduce-scatter.62
  4876.6 42.4 reduce-scatter.64
  4922.2 42.4 reduce-scatter.66
  4968.0 42.4 reduce-scatter.68
  5013.6 42.4 reduce-scatter.70
  (8 shorter events, 175.1 us)
where the time goes:
time: 5090 us; the launch traced here: 5060 us
  matrix products  2760 us (54%)
  waiting for transfers between devices  1060 us (21%)
  local copies, waits for them, and re-layouts  535 us (11%)
  other arithmetic  393 us (8%)
  blocking collectives  274 us (5%)
    dot_general x96, matrix products, block_step(): jnp.einsum('hrgk,rhgd->hkd', attn_prob.astype(jnp.bfloat16), g_blk, prefe...  1190 us
    reduce_scatter x24, waiting for transfers between devices, local_grads(): lax.psum_scatter(dq_part, CP_AXES, scatter_dimension=0, tiled=True)  1020 us
    dot_general x96, matrix products, block_step(): jnp.einsum('hrgk,rhgd->hkd', grad_scores, q_blk, preferred_element_type=j...  592 us
    dot_general x96, matrix products, block_step(): jnp.einsum('rhgd,khd->hrgk', g_blk, value_part, preferred_element_type=jn...  462 us
    dot_general x96, matrix products, block_step(): jnp.einsum('hrgk,khd->rhgd', grad_scores, key_part, preferred_element_typ...  374 us
    add x96, other arithmetic, block_step(): q_pos = row_start + jnp.arange(q_blk.shape[0])  322 us
    dynamic_slice x384, local copies, waits for them, and re-layouts, local_grads(): lax.scan(block_step, (acc_key, acc_value), operands)  303 us
    all_gather x24, blocking collectives, local_grads(): stat_all = lax.all_gather(row_stats[slice_idx], CP_AXES, axis=0, tiled=True)  274 us
  transfers between devices with their start and end apart: 72, of which 24 were waited for; matrix products, arithmetic and copies ran while one was open for 70% of the time, Pallas kernels for 0%

commit v1 on v0

v1 whole, which is shorter than its diff:
```python
import functools
import math

import jax
import jax.numpy as jnp
from jax import lax
from jax.experimental import pallas as pl
from jax.experimental.pallas import tpu as pltpu
from jax.sharding import PartitionSpec as P

CP_AXES = ('cpo', 'cp')
MESH = pl.DeviceIdType.MESH
BF16 = jnp.bfloat16
F32 = jnp.float32

N_DEV = 8
N_SLICES = 24
ROWS_DEV = 8
GROUP = 16
DIM = 128
KEYS = 9728
KEYS_DEV = KEYS // N_DEV
PREFIX = 8192
N_GRP = 3
RB = 1024
CB = 512
NKB = KEYS // CB
CHUNK = 64
SCALE = DIM ** -0.5
EXP_SCALE = SCALE * math.log2(math.e)

PASS_1, PASS_2, PASS_3, PASS_B, N_OUTER = 19, 25, 31, 40, 58


def dg(a, b, ca, cb):
    return lax.dot_general(a, b, (((ca,), (cb,)), ((), ())), preferred_element_type=F32)


def quo(a, b):
    return lax.div(a, jnp.int32(b))


def rem(a, b):
    return lax.rem(a, jnp.int32(b))


def pick(cond, a, b):
    return jnp.where(cond, jnp.int32(a), jnp.int32(b))


def xor3(a, b):
    out = jnp.int32(0)
    for bit in (1, 2, 4):
        out = out + bit * rem(rem(quo(a, bit), 2) + rem(quo(b, bit), 2), 2)
    return out


def kernel(q_h, do_h, st_h, k_h, v_h, dq_o, dk_o, dv_o,
           q_v, do_v, qt_v, dot_v, st_v, kn_v, v_v, kt_v, dqt, dkt, dvt, p0, d0, p1, d1, x_v, okv, odq,
           rows_ss, keys_ss, rows_rs, keys_rs, kv_ss, kv_rs, dq_ss, dq_rs):
    me = lax.axis_index('cpo') * 4 + lax.axis_index('cp')
    chip = quo(me, 2)
    first_kb = 5 * chip

    def dev(e):
        return {'cpo': quo(e, 4), 'cp': rem(e, 4)}

    barrier = pltpu.get_barrier_semaphore()
    for m in range(1, N_DEV):
        pl.semaphore_signal(barrier, inc=1, device_id=dev(xor3(me, jnp.int32(m))), device_id_type=MESH)
    pl.semaphore_wait(barrier, N_DEV - 1)

    def row_copies(m, g):
        e = xor3(me, jnp.int32(m))
        heads = pl.ds(pl.multiple_of(e * GROUP, GROUP), GROUP)
        pairs = ((st_h.at[e, g], st_v.at[m, g], 2),
                 (q_h.at[pl.ds(8 * g, 8), :, heads, :], q_v.at[m, g], 0),
                 (do_h.at[pl.ds(8 * g, 8), :, heads, :], do_v.at[m, g], 1))
        for src, dst, t in pairs:
            if m == 0:
                yield pltpu.make_async_copy(src, dst, rows_rs.at[m, g, t])
            else:
                yield pltpu.make_async_remote_copy(src, dst, rows_ss.at[m, g, t], rows_rs.at[m, g, t],
                                                   device_id=dev(e), device_id_type=MESH)

    def key_copies(e, m, local=False):
        rows = pl.ds(pl.multiple_of(me * KEYS_DEV, CHUNK), KEYS_DEV)
        for src, dst, t in ((k_h.at[e], kn_v.at[rows, :], 0), (v_h.at[e], v_v.at[rows, :], 1)):
            if local:
                yield pltpu.make_async_copy(src, dst, keys_rs.at[m, t])
            else:
                yield pltpu.make_async_remote_copy(src, dst, keys_ss.at[m, t], keys_rs.at[m, t],
                                                   device_id=dev(e), device_id_type=MESH)

    for c in key_copies(me, jnp.int32(0), local=True):
        c.start()
    for c in key_copies(xor3(me, jnp.int32(1)), jnp.int32(1)):
        c.start()
    for g in range(N_GRP):
        for m in (0, 1):
            for c in row_copies(m, g):
                c.start()
    for back in (1, 2, 3):
        for core in (0, 1):
            e = 2 * rem(chip + 4 - back, 4) + core
            for c in key_copies(e, xor3(me, e)):
                c.start()
    for ms in ((2, 3, 4, 5), (6, 7)):
        for g in range(N_GRP):
            for m in ms:
                for c in row_copies(m, g):
                    c.start()

    def zero_keys(i, c):
        dkt[i] = jnp.zeros((DIM, CB), F32)
        dvt[i] = jnp.zeros((DIM, CB), F32)
        return c
    lax.fori_loop(0, NKB, zero_keys, 0)

    def zero_rows(i, c):
        dqt[i] = jnp.zeros((DIM, RB), F32)
        return c
    lax.fori_loop(0, N_DEV * N_GRP, zero_rows, 0)
    p1[...] = jnp.zeros((RB, CB), BF16)
    d1[...] = jnp.zeros((RB, CB), BF16)
    x_v[...] = (lax.broadcasted_iota(jnp.int32, (DIM, CB), 1)
                - lax.broadcasted_iota(jnp.int32, (DIM, CB), 0) // GROUP)

    def tile(kb, m, g, kb_p, rg_p, p_ref, d_ref, pp_ref, dp_ref, masked):
        lane16 = lax.broadcasted_iota(jnp.int32, (DIM, DIM), 1) // 16
        l_rows = lax.broadcasted_iota(jnp.int32, (DIM, CB), 0) % 16
        pick_l = jnp.where(l_rows < 3, 1.0, 0.0).astype(BF16)
        d_lanes = lax.broadcasted_iota(jnp.int32, (CB, DIM), 1) % 16
        pick_d = jnp.where((d_lanes >= 3) & (d_lanes < 6), 1.0, 0.0).astype(BF16)
        keys = pl.ds(pl.multiple_of(kb * CB, CB), CB)
        rhs_s = jnp.concatenate([kt_v[kb], pick_l], axis=0)
        rhs_d = jnp.concatenate([v_v[keys, :], pick_d], axis=1)
        stats = st_v[m, g]
        limit = PREFIX + CB * g + ROWS_DEV * xor3(me, m) - CB * kb

        def scores(rc):
            zero = jnp.zeros((), BF16)
            aug = jnp.concatenate([jnp.where(lane16 == 2 * rc, stats, zero),
                                   jnp.where(lane16 == 2 * rc + 1, stats, zero)], axis=0)
            two = pl.ds(2 * rc, 2)
            s = dg(jnp.concatenate([q_v[m, g, two].reshape(256, DIM), aug], axis=1), rhs_s, 1, 0)
            dp = dg(jnp.concatenate([do_v[m, g, two].reshape(256, DIM), aug], axis=1), rhs_d, 1, 1)
            p = jnp.exp2(s * EXP_SCALE)
            if masked:
                p = jnp.concatenate([jnp.where(x_v[...] <= limit + 64 * (2 * rc), p[:DIM], 0.0),
                                     jnp.where(x_v[...] <= limit + 64 * (2 * rc + 1), p[DIM:], 0.0)], axis=0)
            rows = pl.ds(256 * rc, 256)
            p_ref[rows, :] = p.astype(BF16)
            d_ref[rows, :] = (p * dp).astype(BF16)

        scores(0)
        dvt[kb_p] += dg(dot_v[rg_p], pp_ref[...], 1, 0)
        scores(1)
        dqt[rg_p, :, 0:512] += dg(kt_v[kb_p], dp_ref[0:512, :], 1, 1)
        scores(2)
        dkt[kb_p] += dg(qt_v[rg_p], dp_ref[...], 1, 0)
        scores(3)
        dqt[rg_p, :, 512:1024] += dg(kt_v[kb_p], dp_ref[512:1024, :], 1, 1)

    def flush(kb_p, rg_p):
        dvt[kb_p] += dg(dot_v[rg_p], p1[...], 1, 0)
        dkt[kb_p] += dg(qt_v[rg_p], d1[...], 1, 0)
        dqt[rg_p] += dg(kt_v[kb_p], d1[...], 1, 1)

    def wait_local(ref, sem):
        pltpu.make_async_copy(ref, ref, sem).wait()

    def prepare_rows(m, g):
        wait_local(st_v.at[m, g], rows_rs.at[m, g, 2])
        wait_local(q_v.at[m, g], rows_rs.at[m, g, 0])
        wait_local(do_v.at[m, g], rows_rs.at[m, g, 1])
        rg = m * N_GRP + g
        st_v[m, g] = st_v[m, g].T
        qt_v[rg] = q_v[m, g].reshape(RB, DIM).T
        dot_v[rg] = do_v[m, g].reshape(RB, DIM).T

    def wait_keys(k):
        for core in (0, 1):
            e = 2 * k + core
            m = xor3(me, e)
            rows = pl.ds(pl.multiple_of(e * KEYS_DEV, CHUNK), KEYS_DEV)
            wait_local(kn_v.at[rows, :], keys_rs.at[m, 0])
            wait_local(v_v.at[rows, :], keys_rs.at[m, 1])

    def stage_dq(m, g, par):
        odq[par] = (dqt[m * N_GRP + g].T * SCALE).astype(BF16).reshape(8, ROWS_DEV, GROUP, DIM)

    def send_dq(m, g, par):
        e = xor3(me, m)
        dst = dq_o.at[pl.ds(pl.multiple_of(8 * g, 8), 8), :, pl.ds(pl.multiple_of(me * GROUP, GROUP), GROUP), :]

        @pl.when(m == 0)
        def _():
            pltpu.make_async_copy(odq.at[par], dst, dq_ss.at[par]).start()

        @pl.when(m != 0)
        def _():
            pltpu.make_async_remote_copy(odq.at[par], dst, dq_ss.at[par], dq_rs.at[m],
                                         device_id=dev(e), device_id_type=MESH).start()

    def stage_kv(kb, par):
        okv[par, 0] = dkt[kb].T * SCALE
        okv[par, 1] = dvt[kb].T

    def send_kv(kb, par):
        def piece(j, c):
            ck = 8 * kb + j
            e = quo(ck, KEYS_DEV // CHUNK)
            off = pl.multiple_of(CHUNK * rem(ck, KEYS_DEV // CHUNK), CHUNK)
            m = xor3(me, e)
            src_rows = pl.ds(pl.multiple_of(CHUNK * j, CHUNK), CHUNK)
            for t, out in ((0, dk_o), (1, dv_o)):
                src = okv.at[par, t, src_rows, :]
                dst = out.at[me, pl.ds(off, CHUNK), :]

                @pl.when(m == 0)
                def _():
                    pltpu.make_async_copy(src, dst, kv_ss.at[par, t]).start()

                @pl.when(m != 0)
                def _():
                    pltpu.make_async_remote_copy(src, dst, kv_ss.at[par, t], kv_rs.at[m, t],
                                                 device_id=dev(e), device_id_type=MESH).start()
            return c
        lax.fori_loop(0, CB // CHUNK, piece, 0)

    def wait_kv(par):
        for t in (0, 1):
            wait_local(okv.at[par, t], kv_ss.at[par, t])

    def wait_dq(par):
        wait_local(odq.at[par], dq_ss.at[par])

    def block_of(o):
        i = jnp.where(o < PASS_1, o, jnp.where(o < PASS_2, o - PASS_1 + 4, jnp.where(o < PASS_3, o - PASS_2 + 4, o - PASS_3 + 10)))
        return rem(first_kb + i, NKB)

    def last_rows(n):
        return pick(n < 6, 6, pick(n < 12, 2, 4)) + rem(n, 2), quo(rem(n, 6), 2)

    def outer(o, carry):
        by_rows = o >= PASS_B
        kb = block_of(o)
        m_r, g_r = last_rows(jnp.maximum(o - PASS_B, 0))
        m_lo = pick(o < PASS_1, 0, pick((o >= PASS_2) & (o < PASS_3), 6, 2))
        n_m = pick((o >= PASS_1) & (o < PASS_2), 2, pick((o >= PASS_3), 3, 1))
        g_lo = jnp.maximum(kb - 16, 0)
        count = jnp.where(by_rows, pick((chip == 3) & (g_r == 0), 1, 2), (N_GRP - g_lo) * n_m)
        masked = jnp.where(by_rows, chip == 3, kb >= 16)
        first = (o == 0) | (o == PASS_1) | (o == PASS_2)

        @pl.when(o == 0)
        def _():
            wait_keys(chip)

        new = pick(kb == 0, 0, pick(kb == 4, 1, pick(kb == 9, 2, pick(kb == 14, 3, 4))))

        @pl.when((o < PASS_1) & (new < 4) & (new != chip))
        def _():
            wait_keys(new)

        @pl.when(o < PASS_1)
        def _():
            kt_v[kb] = kn_v[pl.ds(pl.multiple_of(kb * CB, CB), CB), :].T

        def pair(is_masked, j, c):
            kb_p, rg_p = c
            g = jnp.where(by_rows, g_r, g_lo + lax.div(j, n_m))
            m_a = jnp.where(by_rows, m_r, m_lo + 2 * lax.rem(j, n_m))
            m_b = jnp.where(by_rows, m_r, m_a + 1)
            kb_a = jnp.where(by_rows, first_kb + 2 * j, kb)
            kb_b = jnp.where(by_rows, first_kb + 2 * j + 1, kb)
            if not is_masked:
                @pl.when(first)
                def _():
                    prepare_rows(m_a, g)
                    prepare_rows(m_b, g)
            tile(kb_a, m_a, g, kb_p, rg_p, p0, d0, p1, d1, is_masked)
            tile(kb_b, m_b, g, kb_a, m_a * N_GRP + g, p1, d1, p0, d0, is_masked)
            return kb_b, m_b * N_GRP + g

        carry = lax.fori_loop(0, jnp.where(masked, 0, count), functools.partial(pair, False), carry)
        carry = lax.fori_loop(0, jnp.where(masked, count, 0), functools.partial(pair, True), carry)

        par = rem(o, 2)
        own = (o >= PASS_1 + 1) & (o < PASS_1 + 7)
        late = o >= PASS_B + 1
        r = o - (PASS_1 + 1)
        m_l, g_l = last_rows(jnp.maximum(o - PASS_B - 1, 0))
        m_s = jnp.where(own, rem(jnp.maximum(r, 0), 2), m_l)
        g_s = jnp.where(own, quo(jnp.maximum(r, 0), 2), g_l)

        own_b = (o >= PASS_1 + 2) & (o < PASS_1 + 8)
        m_l, g_l = last_rows(jnp.maximum(o - PASS_B - 2, 0))
        m_t = jnp.where(own_b, rem(jnp.maximum(r - 1, 0), 2), m_l)
        g_t = jnp.where(own_b, quo(jnp.maximum(r - 1, 0), 2), g_l)

        @pl.when(own_b | (o >= PASS_B + 2))
        def _():
            send_dq(m_t, g_t, 1 - par)

        @pl.when((o >= PASS_2 + 2) & (o <= PASS_B + 1))
        def _():
            send_kv(block_of(o - 2), 1 - par)

        @pl.when((own & (o >= PASS_1 + 3)) | late)
        def _():
            wait_dq(par)

        @pl.when(own | late)
        def _():
            stage_dq(m_s, g_s, par)

        @pl.when((o >= PASS_2 + 3) & (o <= PASS_B))
        def _():
            wait_kv(par)

        @pl.when((o >= PASS_2 + 1) & (o <= PASS_B))
        def _():
            stage_kv(block_of(o - 1), par)
        return carry

    m_0 = jnp.int32(0)
    kb_p, rg_p = lax.fori_loop(0, N_OUTER, outer, (first_kb, m_0))
    flush(kb_p, rg_p)

    m_t, g_t = last_rows(jnp.int32(16))
    m_s, g_s = last_rows(jnp.int32(17))
    end = N_OUTER % 2
    send_dq(m_t, g_t, 1 - end)
    wait_dq(end)
    stage_dq(m_s, g_s, end)

    def last_blocks(i, c):
        par = rem(i, 2)

        @pl.when(i > 0)
        def _():
            send_kv(first_kb + i - 1, 1 - par)

        @pl.when(i < 4)
        def _():
            wait_kv(par)
            stage_kv(first_kb + i, par)
        return c
    lax.fori_loop(0, 5, last_blocks, 0)
    send_dq(m_s, g_s, end)

    for par in (0, 1):
        wait_dq(par)
        wait_kv(par)
    for m in range(1, N_DEV):
        for g in range(N_GRP):
            wait_local(st_v.at[m, g], rows_ss.at[m, g, 2])
            wait_local(q_v.at[m, g], rows_ss.at[m, g, 0])
            wait_local(do_v.at[m, g], rows_ss.at[m, g, 1])
        wait_local(kn_v.at[pl.ds(0, KEYS_DEV), :], keys_ss.at[m, 0])
        wait_local(v_v.at[pl.ds(0, KEYS_DEV), :], keys_ss.at[m, 1])
        heads = pl.ds(0, GROUP)
        wait_local(dq_o.at[:, :, heads, :], dq_rs.at[m])
        wait_local(dk_o.at[0], kv_rs.at[m, 0])
        wait_local(dv_o.at[0], kv_rs.at[m, 1])


def split3(x):
    hi = lax.reduce_precision(x, 8, 7)
    mid = lax.reduce_precision(x - hi, 8, 7)
    lo = (x - hi) - mid
    return [hi, mid, lo]


def solution(mesh):
    row_spec = P(None, CP_AXES, 'heads', None)
    stat_spec = P(None, CP_AXES, 'heads')
    key_spec = P(CP_AXES, 'heads', None)
    any_ = pl.BlockSpec(memory_space=pl.ANY)

    def local_grads(queries, attn_out, grad_out, log_sum_exp, key_cache, value_cache):
        row_delta = jnp.sum(grad_out.astype(F32) * attn_out.astype(F32), axis=-1)
        parts = split3(log_sum_exp * (-1.0 / SCALE)) + split3(-row_delta)
        parts = parts + [jnp.zeros_like(row_delta)] * 10
        stats = jnp.stack(parts, axis=0).astype(BF16)
        stats = stats.reshape(16, N_GRP, 8, ROWS_DEV, N_DEV, GROUP)
        stats = jnp.transpose(stats, (4, 1, 2, 0, 3, 5)).reshape(N_DEV, N_GRP, DIM, DIM)
        keys = jnp.transpose(key_cache, (1, 0, 2))
        values = jnp.transpose(value_cache, (1, 0, 2))
        dma = pltpu.SemaphoreType.DMA
        rows_shape = (N_DEV, N_GRP, 8, ROWS_DEV, GROUP, DIM)
        n_rg = N_DEV * N_GRP
        grad_query, grad_key, grad_value = pl.pallas_call(
            kernel,
            name='attn_bwd',
            out_shape=(jax.ShapeDtypeStruct((N_SLICES, ROWS_DEV, N_DEV * GROUP, DIM), BF16),
                       jax.ShapeDtypeStruct((N_DEV, KEYS_DEV, DIM), F32),
                       jax.ShapeDtypeStruct((N_DEV, KEYS_DEV, DIM), F32)),
            in_specs=[any_] * 5,
            out_specs=[any_] * 3,
            scratch_shapes=[
                pltpu.VMEM(rows_shape, BF16), pltpu.VMEM(rows_shape, BF16),
                pltpu.VMEM((n_rg, DIM, RB), BF16), pltpu.VMEM((n_rg, DIM, RB), BF16),
                pltpu.VMEM((N_DEV, N_GRP, DIM, DIM), BF16),
                pltpu.VMEM((KEYS, DIM), BF16), pltpu.VMEM((KEYS, DIM), BF16),
                pltpu.VMEM((NKB, DIM, CB), BF16),
                pltpu.VMEM((n_rg, DIM, RB), F32),
                pltpu.VMEM((NKB, DIM, CB), F32), pltpu.VMEM((NKB, DIM, CB), F32),
                pltpu.VMEM((RB, CB), BF16), pltpu.VMEM((RB, CB), BF16),
                pltpu.VMEM((RB, CB), BF16), pltpu.VMEM((RB, CB), BF16),
                pltpu.VMEM((DIM, CB), jnp.int32),
                pltpu.VMEM((2, 2, CB, DIM), F32),
                pltpu.VMEM((2, 8, ROWS_DEV, GROUP, DIM), BF16),
                dma((N_DEV, N_GRP, 3)), dma((N_DEV, 2)), dma((N_DEV, N_GRP, 3)), dma((N_DEV, 2)),
                dma((2, 2)), dma((N_DEV, 2)), dma((2,)), dma((N_DEV,)),
            ],
            compiler_params=pltpu.CompilerParams(collective_id=0, has_side_effects=True, vmem_limit_bytes=67043328),
        )(queries, grad_out, stats, keys, values)
        return grad_query, jnp.transpose(grad_key, (1, 0, 2)), jnp.transpose(grad_value, (1, 0, 2))

    return jax.shard_map(local_grads, mesh=mesh, in_specs=(row_spec, row_spec, row_spec, stat_spec, key_spec, key_spec),
                         out_specs=(row_spec, key_spec, key_spec), check_vma=False)
```

time: 5090 us -> 663 us (0.13)
  matrix products: 2760 us -> 0 us
  waiting for transfers between devices: 1060 us -> 0 us
  Pallas kernels: 0 us -> 603 us
  local copies, waits for them, and re-layouts: 535 us -> 44.4 us
  other arithmetic: 393 us -> 8.45 us
  blocking collectives: 274 us -> 0 us
    dot_general x480 -> x0, matrix products: 2760 us -> none  [the longest x96 1190 us: block_step(): jnp.einsum('hrgk,rhgd->hkd', attn_prob.astype(jnp.bfloat16), g_blk, prefe...]
    reduce_scatter x24 -> x0, waiting for transfers between devices: 1020 us -> none  [local_grads(): lax.psum_scatter(dq_part, CP_AXES, scatter_dimension=0, tiled=True)]
    pallas_call x0 -> x1, Pallas kernels: none -> 603 us  [local_grads(): pl.pallas_call(kernel, name='attn_bwd', out_shape=(jax.ShapeDtypeStruct((...]
    add x216 -> x0, other arithmetic: 334 us -> none  [the longest x96 322 us: block_step(): q_pos = row_start + jnp.arange(q_blk.shape[0])]
    dynamic_slice x384 -> x0, local copies, waits for them, and re-layouts: 303 us -> none  [local_grads(): lax.scan(block_step, (acc_key, acc_value), operands)]
    all_gather x24 -> x0, blocking collectives: 274 us -> none  [local_grads(): stat_all = lax.all_gather(row_stats[slice_idx], CP_AXES, axis=0, tiled=True)]
    dynamic_update_slice x96 -> x0, local copies, waits for them, and re-layouts: 107 us -> none  [local_grads(): lax.scan(block_step, (acc_key, acc_value), operands)]
    another operation x24 -> x4, local copies, waits for them, and re-layouts: 60.5 us -> 5.55 us  [local_grads(): stats = jnp.stack(parts, axis=0).astype(BF16)]
  transfers between devices with their start and end apart: 72 -> 0, of which waited for: 24 -> 0; matrix products, arithmetic and copies ran while one was open for 70% -> 0% of each run, Pallas kernels for 0% -> 0%
where the time goes in v1:
time: 663 us; the launch traced here: 657 us
  Pallas kernels  603 us (91%)
  local copies, waits for them, and re-layouts  44.4 us (7%)
  other arithmetic  8.45 us (1%)
    pallas_call x1, Pallas kernels, local_grads(): pl.pallas_call(kernel, name='attn_bwd', out_shape=(jax.ShapeDtypeStruct((...  603 us
    unnamed x26, local copies, waits for them, and re-layouts  25.8 us

profile of v1, /device:TPU:0, one launch (start us, length us, event | category | flops | bytes accessed | tf_op | source)
XLA Modules:
  0.0 657.0 jit_solution(14988920508281724540)
XLA Ops:
  0.6 0.0 copy-start.1
  0.6 0.0 copy-start.5
  0.7 8.1 %multiply_reduce_fusion = f32[24,8,128]{2,1,0:T(8,128)S(1)} fusion(bf16[24,8,128,128]{3,2,1,0:T(8,128)(2,1)} %param.7, bf16[24,8,128,128]{3,2,1,0:T(8,128)(2,1)} %do_h.1), kind=kLoop, calls=%fused_computation | loop fusion | flops 12558336 | bytes 12681216 | tf_op jit(solution)/shard_map/reduce_sum | solution.py:384
  8.8 0.0 copy-done.5
  8.8 1.0 stack.23
  9.8 1.0 stack.22
  10.9 1.0 stack.21
  11.9 0.2 neg.25
  12.2 0.0 copy-start.4
  12.2 0.0 copy-start.3
  12.2 0.0 copy-start.2
  12.2 0.3 fusion
  12.5 0.0 copy-done.1
  12.5 4.9 copy_bitcast_fusion
  17.4 0.0 copy-done.4
  17.4 0.8 copy_dynamic-update-slice_fusion.5
  18.2 0.0 copy-done.3
  18.2 0.8 copy_dynamic-update-slice_fusion.4
  19.1 0.0 copy-done.2
  19.1 0.8 copy_dynamic-update-slice_fusion.3
  19.9 0.8 copy_dynamic-update-slice_fusion.2
  20.7 0.8 copy_dynamic-update-slice_fusion.1
  21.6 0.8 copy_dynamic-update-slice_fusion
  22.4 1.0 broadcast_dynamic-update-slice_fusion.1
  23.5 2.5 broadcast_dynamic-update-slice_fusion
  25.9 7.9 %reshape.57.st_h = bf16[8,3,128,128]{3,2,1,0:T(8,128)(2,1)} reshape(bf16[8,3,8,16,8,16]{5,4,3,2,1,0:T(8,128)(2,1)} %bitcast) | data formatting | bytes 1572864 | tf_op jit(solution)/shard_map/reshape | solution.py:389
  33.8 603.4 %attn_bwd.1 = (bf16[24,8,128,128]{3,2,1,0:T(8,128)(2,1)}, f32[8,1216,128]{2,1,0:T(8,128)}, f32[8,1216,128]{2,1,0:T(8,128)}) custom-call(bf16[24,8,128,128]{3,2,1,0:T(8,128)(2,1)} %q_h.1, bf16[24,8,128,128]{3,2,1,0:T(8,128)(2,1)} %do_h.1, bf16[8,3,128,128]{3,2,1,0:T(8,128)(2,1)} %reshape.57.st_h, bf16[8,1216,128]{2,1,0:T(8,128)(2,1)} %get-tuple-element.22.k_h, ...), custom_call_target="tpu_custom_call" | custom-call | tf_op jit(solution)/shard_map/attn_bwd/pallas_call | solution.py:395
  637.2 0.0 copy-start
  637.2 0.0 slice-start
  637.3 9.1 %copy.24 = f32[1216,8,128]{2,1,0:T(8,128)} copy(f32[1216,8,128]{2,0,1:T(8,128)} %bitcast.12) | data formatting | bytes 9961472
  646.4 0.0 copy-done
  646.4 0.0 slice-start.1
  646.4 7.9 %copy.25 = f32[1216,8,128]{2,1,0:T(8,128)} copy(f32[1216,8,128]{2,0,1:T(8,128)S(1)} %bitcast.11) | data formatting | bytes 9961472
  654.3 0.0 slice-done
  654.3 0.0 slice-done.1
  654.3 2.7 copy.42
  (3 shorter events, 0.0 us)
Async XLA Ops:
  0.6 11.9 %copy-start.1 = (bf16[1216,8,128]{2,1,0:T(8,128)(2,1)S(1)}, bf16[1216,8,128]{2,1,0:T(8,128)(2,1)}, u32[]{:S(2)}) copy-start(bf16[1216,8,128]{2,1,0:T(8,128)(2,1)} %param.11) | copy-start | bytes 7471108
  0.6 8.1 %copy-start.5 = (f32[24,8,128]{2,1,0:T(8,128)S(1)}, f32[24,8,128]{2,1,0:T(8,128)}, u32[]{:S(2)}) copy-start(f32[24,8,128]{2,1,0:T(8,128)} %param.9) | copy-start | bytes 294916
  12.2 5.2 copy-start.4
  12.2 6.0 copy-start.3
  12.2 6.9 %copy-start.2 = (bf16[1,3,8,8,8,16]{5,4,3,2,1,0:T(8,128)(2,1)S(1)}, bf16[1,3,8,8,8,16]{5,4,3,2,1,0:T(8,128)(2,1)}, u32[]{:S(2)}) copy-start(bf16[1,3,8,8,8,16]{5,4,3,2,1,0:T(8,128)(2,1)} %stack.23) | copy-start | bytes 147460
  637.2 9.1 %copy-start = (f32[8,1216,128]{2,1,0:T(8,128)S(1)}, f32[8,1216,128]{2,1,0:T(8,128)}, u32[]{:S(2)}) copy-start(f32[8,1216,128]{2,1,0:T(8,128)} %get-tuple-element.8) | copy-start | bytes 14942212
  637.2 17.0 %slice-start = ((s8[6291456]{0:T(1024)(128)(4,1)}), s8[4194304]{0:T(1024)(128)(4,1)S(1)}, s32[]{:S(2)}) async-start(s8[6291456]{0:T(1024)(128)(4,1)} %bitcast.9), calls=%async_computation | async-start | bytes 8388608
  646.4 7.9 %slice-start.1 = ((s8[6291456]{0:T(1024)(128)(4,1)}), s8[2097152]{0:T(1024)(128)(4,1)S(1)}, s32[]{:S(2)}) async-start(s8[6291456]{0:T(1024)(128)(4,1)} %bitcast.9), calls=%async_computation.1 | async-start | bytes 4194304

commit v2 on v1

v2 whole, which is shorter than its diff:
```python
import functools
import math

import jax
import jax.numpy as jnp
from jax import lax
from jax.experimental import pallas as pl
from jax.experimental.pallas import tpu as pltpu
from jax.sharding import PartitionSpec as P

CP_AXES = ('cpo', 'cp')
MESH = pl.DeviceIdType.MESH
BF16 = jnp.bfloat16
F32 = jnp.float32

N_DEV = 8
N_SLICES = 24
ROWS_DEV = 8
GROUP = 16
DIM = 128
KEYS = 9728
KEYS_DEV = KEYS // N_DEV
PREFIX = 8192
N_GRP = 3
RB = 1024
CB = 512
NKB = KEYS // CB
CHUNK = 64
SCALE = DIM ** -0.5
EXP_SCALE = SCALE * math.log2(math.e)

UNROLL = 6
N_BUF = 3

PASS_1, PASS_2, PASS_D, PASS_3, PASS_B, PASS_C, N_OUTER = 17, 23, 38, 40, 49, 53, 54


def dg(a, b, ca, cb):
    return lax.dot_general(a, b, (((ca,), (cb,)), ((), ())), preferred_element_type=F32)


def quo(a, b):
    return lax.div(a, jnp.int32(b))


def rem(a, b):
    return lax.rem(a, jnp.int32(b))


def pick(cond, a, b):
    return jnp.where(cond, jnp.int32(a), jnp.int32(b))


def xor3(a, b):
    out = jnp.int32(0)
    for bit in (1, 2, 4):
        out = out + bit * rem(rem(quo(a, bit), 2) + rem(quo(b, bit), 2), 2)
    return out


def kernel(q_h, do_h, st_h, k_h, v_h, dq_o, dk_o, dv_o,
           q_v, do_v, qt_v, dot_v, st_v, aug_v, k_v, v_v, dqt, dkt, dvt, p0, d0, p1, d1, x_v, okv, odq,
           rows_ss, keys_ss, rows_rs, keys_rs, kv_ss, kv_rs, dq_ss, dq_rs):
    me = lax.axis_index('cpo') * 4 + lax.axis_index('cp')
    chip = quo(me, 2)
    first_kb = 5 * chip

    def dev(e):
        return {'cpo': quo(e, 4), 'cp': rem(e, 4)}

    barrier = pltpu.get_barrier_semaphore()
    for m in range(1, N_DEV):
        pl.semaphore_signal(barrier, inc=1, device_id=dev(xor3(me, jnp.int32(m))), device_id_type=MESH)

    def zero_keys(i, c):
        dkt[i] = jnp.zeros((DIM, CB), F32)
        dvt[i] = jnp.zeros((DIM, CB), F32)
        return c
    lax.fori_loop(0, NKB, zero_keys, 0)

    def zero_rows(i, c):
        dqt[i] = jnp.zeros((DIM, RB), F32)
        return c
    lax.fori_loop(0, N_DEV * N_GRP, zero_rows, 0)
    p1[...] = jnp.zeros((RB, CB), BF16)
    d1[...] = jnp.zeros((RB, CB), BF16)
    x_v[...] = (lax.broadcasted_iota(jnp.int32, (DIM, CB), 1)
                - lax.broadcasted_iota(jnp.int32, (DIM, CB), 0) // GROUP)

    pl.semaphore_wait(barrier, N_DEV - 1)

    def row_copies(m, g):
        e = xor3(me, jnp.int32(m))
        heads = pl.ds(pl.multiple_of(e * GROUP, GROUP), GROUP)
        pairs = ((st_h.at[e, g], st_v.at[m, g], 2),
                 (q_h.at[pl.ds(8 * g, 8), :, heads, :], q_v.at[m, g], 0),
                 (do_h.at[pl.ds(8 * g, 8), :, heads, :], do_v.at[m, g], 1))
        for src, dst, t in pairs:
            if m == 0:
                yield pltpu.make_async_copy(src, dst, rows_rs.at[m, g, t])
            else:
                yield pltpu.make_async_remote_copy(src, dst, rows_ss.at[m, g, t], rows_rs.at[m, g, t],
                                                   device_id=dev(e), device_id_type=MESH)

    def key_copies(e, m, local=False):
        rows = pl.ds(pl.multiple_of(me * KEYS_DEV, CHUNK), KEYS_DEV)
        for src, dst, t in ((k_h.at[e], k_v.at[rows, :], 0), (v_h.at[e], v_v.at[rows, :], 1)):
            if local:
                yield pltpu.make_async_copy(src, dst, keys_rs.at[m, t])
            else:
                yield pltpu.make_async_remote_copy(src, dst, keys_ss.at[m, t], keys_rs.at[m, t],
                                                   device_id=dev(e), device_id_type=MESH)

    for c in key_copies(me, jnp.int32(0), local=True):
        c.start()
    for c in key_copies(xor3(me, jnp.int32(1)), jnp.int32(1)):
        c.start()
    for g in range(N_GRP):
        for m in (0, 1):
            for c in row_copies(m, g):
                c.start()
    for back in (1, 2, 3):
        for core in (0, 1):
            e = 2 * rem(chip + 4 - back, 4) + core
            for c in key_copies(e, xor3(me, e)):
                c.start()
    for ms in ((2, 3, 4, 5), (6, 7)):
        for g in range(N_GRP):
            for m in ms:
                for c in row_copies(m, g):
                    c.start()

    def keys_t(ref, kb):
        return jnp.concatenate([ref[pl.ds(pl.multiple_of(kb * CB + DIM * i, DIM), DIM), :] for i in range(CB // DIM)], axis=1)

    def tile(kb, m, g, kb_p, rg_p, p_ref, d_ref, pp_ref, dp_ref, masked):
        slice_of = lax.broadcasted_iota(jnp.int32, (DIM, DIM), 1) % 8
        part_row = lax.broadcasted_iota(jnp.int32, (DIM, CB), 0)
        pick_l = jnp.where(part_row < 24, 1.0, 0.0).astype(BF16)
        pick_d = jnp.where((part_row >= 24) & (part_row < 48), 1.0, 0.0).astype(BF16)
        rhs_s = jnp.concatenate([keys_t(k_v, kb), pick_l], axis=0)
        rhs_d = jnp.concatenate([keys_t(v_v, kb), pick_d], axis=0)
        stats = aug_v[m, g]
        limit = PREFIX + CB * g + ROWS_DEV * xor3(me, m) - CB * kb

        def lhs(ref, rc):
            zero = jnp.zeros((), BF16)
            aug = jnp.concatenate([jnp.where(slice_of == 2 * rc, stats, zero),
                                   jnp.where(slice_of == 2 * rc + 1, stats, zero)], axis=0)
            return jnp.concatenate([ref[m, g, pl.ds(2 * rc, 2)].reshape(256, DIM), aug], axis=1)

        def score(rc):
            return dg(lhs(q_v, rc), rhs_s, 1, 0)

        def grad(rc):
            return dg(lhs(do_v, rc), rhs_d, 1, 0)

        def finish(rc, s, dp):
            p = jnp.exp2(s * EXP_SCALE)
            if masked:
                p = jnp.concatenate([jnp.where(x_v[...] <= limit + 64 * (2 * rc), p[:DIM], 0.0),
                                     jnp.where(x_v[...] <= limit + 64 * (2 * rc + 1), p[DIM:], 0.0)], axis=0)
            rows = pl.ds(256 * rc, 256)
            p_ref[rows, :] = p.astype(BF16)
            d_ref[rows, :] = (p * dp).astype(BF16)

        def dq_half(h, k):
            cols = slice(256 * k, 256 * k + 256)
            return dg(keys_t(k_v, kb_p)[:, cols], dp_ref[512 * h:512 * h + 512, cols], 1, 1)

        def dv_part(i):
            return dg(dot_v[rg_p][:, 256 * i:256 * i + 256], pp_ref[256 * i:256 * i + 256, :], 1, 0)

        def dk_part(i):
            return dg(qt_v[rg_p][:, 256 * i:256 * i + 256], dp_ref[256 * i:256 * i + 256, :], 1, 0)

        def put_dq(h, x):
            dqt[rg_p, :, 512 * h:512 * h + 512] = x + dqt[rg_p, :, 512 * h:512 * h + 512]

        s = score(0)
        dq = dq_half(0, 0)
        dp = grad(0)
        finish(0, s, dp)
        put_dq(0, dq_half(0, 1) + dq)
        s = score(1)
        dv = dv_part(0)
        dv = dv_part(1) + dv
        dp = grad(1)
        finish(1, s, dp)
        dv = dv_part(2) + dv
        dv = dv_part(3) + dv
        dvt[kb_p] = dv + dvt[kb_p]
        s = score(2)
        dq = dq_half(1, 0)
        dp = grad(2)
        finish(2, s, dp)
        put_dq(1, dq_half(1, 1) + dq)
        s = score(3)
        dk = dk_part(0)
        dk = dk_part(1) + dk
        dp = grad(3)
        finish(3, s, dp)
        dk = dk_part(2) + dk
        dk = dk_part(3) + dk
        dkt[kb_p] = dk + dkt[kb_p]

    def flush(kb_p, rg_p):
        dvt[kb_p] += dg(dot_v[rg_p], p1[...], 1, 0)
        dkt[kb_p] += dg(qt_v[rg_p], d1[...], 1, 0)
        dqt[rg_p] += dg(keys_t(k_v, kb_p), d1[...], 1, 1)

    def wait_local(ref, sem):
        pltpu.make_async_copy(ref, ref, sem).wait()

    def prepare_rows(m, g):
        wait_local(st_v.at[m, g], rows_rs.at[m, g, 2])
        wait_local(q_v.at[m, g], rows_rs.at[m, g, 0])
        wait_local(do_v.at[m, g], rows_rs.at[m, g, 1])
        rg = m * N_GRP + g
        x = st_v[m, g]
        hi = x.astype(BF16).astype(F32)
        mid = (x - hi).astype(BF16).astype(F32)
        lo = (x - hi) - mid
        parts = [y[8 * t:8 * t + 8] for t in (0, 1) for y in (hi, mid, lo)]
        aug_v[m, g] = jnp.concatenate(parts + [jnp.zeros((80, DIM), F32)], axis=0).T.astype(BF16)
        qt_v[rg] = q_v[m, g].reshape(RB, DIM).T
        dot_v[rg] = do_v[m, g].reshape(RB, DIM).T

    def wait_keys(k):
        for core in (0, 1):
            e = 2 * k + core
            m = xor3(me, e)
            rows = pl.ds(pl.multiple_of(e * KEYS_DEV, CHUNK), KEYS_DEV)
            wait_local(k_v.at[rows, :], keys_rs.at[m, 0])
            wait_local(v_v.at[rows, :], keys_rs.at[m, 1])

    def prepare_keys(kb):
        for i in range(CB // DIM):
            rows = pl.ds(pl.multiple_of(kb * CB + DIM * i, DIM), DIM)
            k_v[rows, :] = k_v[rows, :].T
            v_v[rows, :] = v_v[rows, :].T

    def stage_dq(m, par):
        for g in range(N_GRP):
            odq[par, g] = (dqt[m * N_GRP + g].T * SCALE).astype(BF16).reshape(8, ROWS_DEV, GROUP, DIM)

    def send_dq(m, par):
        e = xor3(me, m)
        heads = pl.ds(pl.multiple_of(me * GROUP, GROUP), GROUP)
        for g in range(N_GRP):
            dst = dq_o.at[pl.ds(8 * g, 8), :, heads, :]

            @pl.when(m == 0)
            def _():
                pltpu.make_async_copy(odq.at[par, g], dst, dq_ss.at[par, g]).start()

            @pl.when(m != 0)
            def _():
                pltpu.make_async_remote_copy(odq.at[par, g], dst, dq_ss.at[par, g], dq_rs.at[m],
                                             device_id=dev(e), device_id_type=MESH).start()

    def stage_kv(kb, buf):
        okv[buf, 0] = dkt[kb].T * SCALE
        okv[buf, 1] = dvt[kb].T

    def send_kv(kb, buf):
        def piece(j, c):
            ck = 8 * kb + j
            e = quo(ck, KEYS_DEV // CHUNK)
            off = pl.multiple_of(CHUNK * rem(ck, KEYS_DEV // CHUNK), CHUNK)
            m = xor3(me, e)
            src_rows = pl.ds(pl.multiple_of(CHUNK * j, CHUNK), CHUNK)
            for t, out in ((0, dk_o), (1, dv_o)):
                src = okv.at[buf, t, src_rows, :]
                dst = out.at[me, pl.ds(off, CHUNK), :]

                @pl.when(m == 0)
                def _():
                    pltpu.make_async_copy(src, dst, kv_ss.at[buf, t]).start()

                @pl.when(m != 0)
                def _():
                    pltpu.make_async_remote_copy(src, dst, kv_ss.at[buf, t], kv_rs.at[m, t],
                                                 device_id=dev(e), device_id_type=MESH).start()
            return c
        lax.fori_loop(0, CB // CHUNK, piece, 0)

    def wait_kv(buf):
        for t in (0, 1):
            wait_local(okv.at[buf, t], kv_ss.at[buf, t])

    def wait_dq(par):
        for g in range(N_GRP):
            wait_local(odq.at[par, g], dq_ss.at[par, g])

    def between(o, lo, hi):
        return (o >= lo) & (o < hi)

    def block_of(o):
        n = jnp.where(o < PASS_2, o - PASS_1, jnp.where(o < PASS_D, o - PASS_2, o - PASS_3 + 6))
        n = jnp.maximum(n, 0)
        other = 4 + 5 * rem(n, 3) + quo(n, 3)
        i = jnp.where(o < PASS_1, jnp.where(o < 2, o, o + 2), other)
        return rem(first_kb + i, NKB)

    def rows_of(o):
        n = jnp.maximum(o - PASS_B, 0)
        return jnp.where(o < PASS_B, 6 + o - PASS_D, 2 + 2 * rem(n, 2) + quo(n, 2))

    def kv_event(o):
        return jnp.where(o < PASS_D, o - PASS_2, 6 + o - PASS_3)

    def outer(o, carry):
        ends = between(o, PASS_D, PASS_3) | between(o, PASS_B, PASS_C)
        last = o >= PASS_C
        kb = block_of(o)
        m_r = rows_of(o)
        m_lo = pick(o < PASS_1, 0, pick(between(o, PASS_2, PASS_D), 6, 2))
        n_m = pick((o < PASS_1) | between(o, PASS_2, PASS_D), 2, 4)
        g_lo = jnp.maximum(kb - 16, 0)
        masked = jnp.where(ends | last, chip == 3, kb >= 16)
        n_full = jnp.where(ends | last, 2, quo(n_m, 2))
        n_pairs = jnp.where(ends, 5, jnp.where(last, 4, (N_GRP - g_lo) * quo(n_m, 2)))
        first = (o == 0) | (o == PASS_1) | (o == PASS_2)

        @pl.when(o == 0)
        def _():
            wait_keys(chip)

        new = pick(kb == 0, 0, pick(kb == 4, 1, pick(kb == 9, 2, pick(kb == 14, 3, 4))))

        @pl.when((o < PASS_1) & (new < 4) & (new != chip))
        def _():
            wait_keys(new)

        @pl.when(o < PASS_1)
        def _():
            prepare_keys(kb)

        @pl.when(o < 2)
        def _():
            prepare_keys(kb + 2)

        def index(n):
            g = jnp.where(ends | last, quo(n, 4), lax.div(n, n_m))
            m = jnp.where(ends, m_r, jnp.where(last, rem(quo(n, 2), 2), m_lo + lax.rem(n, n_m)))
            k = jnp.where(ends, first_kb + rem(n, 4), jnp.where(last, first_kb + 2 + rem(n, 2), kb))
            return k, m, g

        def six(j, c):
            @pl.when(first)
            def _():
                def one(t, c):
                    _, m, g = index(UNROLL * j + t)
                    prepare_rows(m, g)
                    return c
                lax.fori_loop(0, UNROLL, one, 0)
            kb_p, rg_p = c
            for t in range(UNROLL):
                k, m, g = index(UNROLL * j + t)
                bufs = (p0, d0, p1, d1) if t % 2 == 0 else (p1, d1, p0, d0)
                tile(k, m, g, kb_p, rg_p, *bufs, False)
                kb_p, rg_p = k, m * N_GRP + g
            return kb_p, rg_p

        def pair(j, c):
            kb_p, rg_p = c
            n2 = quo(n_m, 2)
            g = jnp.where(ends, quo(j + 1, 2), jnp.where(last, 1 + quo(j, 2), g_lo + lax.div(j, n2)))
            half = jnp.where(ends, jnp.where(j == 0, 0, rem(j + 1, 2)), 1)
            m_a = jnp.where(ends, m_r, jnp.where(last, rem(j, 2), m_lo + 2 * lax.rem(j, n2)))
            m_b = jnp.where(ends | last, m_a, m_a + 1)
            k_a = jnp.where(ends | last, first_kb + 2 * half, kb)
            k_b = jnp.where(ends | last, k_a + 1, kb)
            tile(k_a, m_a, g, kb_p, rg_p, p0, d0, p1, d1, True)
            tile(k_b, m_b, g, k_a, m_a * N_GRP + g, p1, d1, p0, d0, True)
            return k_b, m_b * N_GRP + g

        carry = lax.fori_loop(0, jnp.where(masked, 0, n_full), six, carry)
        carry = lax.fori_loop(0, jnp.where(masked, n_pairs, 0), pair, carry)

        par = rem(o, 2)

        @pl.when(between(o, PASS_D + 2, PASS_3 + 2) | between(o, PASS_B + 2, PASS_C + 2))
        def _():
            send_dq(rows_of(o - 2), 1 - par)

        @pl.when(between(o, PASS_2 + 2, PASS_2 + 8) | between(o, PASS_3 + 2, PASS_B + 2))
        def _():
            send_kv(block_of(o - 2), rem(kv_event(o - 2), N_BUF))

        @pl.when(between(o, PASS_D + 1, PASS_3 + 1) | between(o, PASS_B + 1, PASS_C + 1))
        def _():
            @pl.when(o > PASS_3)
            def _():
                wait_dq(par)
            stage_dq(rows_of(o - 1), par)

        @pl.when(between(o, PASS_2 + 1, PASS_2 + 7) | between(o, PASS_3 + 1, PASS_B + 1))
        def _():
            ev = kv_event(o - 1)

            @pl.when(ev >= N_BUF)
            def _():
                wait_kv(rem(ev, N_BUF))
            stage_kv(block_of(o - 1), rem(ev, N_BUF))
        return carry

    kb_p, rg_p = lax.fori_loop(0, N_OUTER, outer, (first_kb, jnp.int32(0)))
    flush(kb_p, rg_p)

    send_dq(rows_of(jnp.int32(PASS_C - 1)), (N_OUTER - 1) % 2)

    def last_parts(i, c):
        @pl.when((i > 0) & (i < 5))
        def _():
            send_kv(first_kb + i - 1, rem(14 + i, N_BUF))

        @pl.when(i < 4)
        def _():
            wait_kv(rem(15 + i, N_BUF))
            stage_kv(first_kb + i, rem(15 + i, N_BUF))

        @pl.when(i > 1)
        def _():
            par = rem(i, 2)

            @pl.when(i < 4)
            def _():
                wait_dq(par)
                stage_dq(i - 2, par)

            @pl.when(i > 2)
            def _():
                send_dq(i - 3, 1 - par)
        return c
    lax.fori_loop(0, 5, last_parts, 0)

    for par in (0, 1):
        wait_dq(par)
    for buf in range(N_BUF):
        wait_kv(buf)
    for m in range(1, N_DEV):
        for g in range(N_GRP):
            wait_local(st_v.at[m, g], rows_ss.at[m, g, 2])
            wait_local(q_v.at[m, g], rows_ss.at[m, g, 0])
            wait_local(do_v.at[m, g], rows_ss.at[m, g, 1])
        wait_local(k_v.at[pl.ds(0, KEYS_DEV), :], keys_ss.at[m, 0])
        wait_local(v_v.at[pl.ds(0, KEYS_DEV), :], keys_ss.at[m, 1])
        heads = pl.ds(0, GROUP)
        wait_local(dq_o.at[:, :, heads, :], dq_rs.at[m])
        wait_local(dk_o.at[0], kv_rs.at[m, 0])
        wait_local(dv_o.at[0], kv_rs.at[m, 1])


def solution(mesh):
    row_spec = P(None, CP_AXES, 'heads', None)
    stat_spec = P(None, CP_AXES, 'heads')
    key_spec = P(CP_AXES, 'heads', None)
    any_ = pl.BlockSpec(memory_space=pl.ANY)

    def local_grads(queries, attn_out, grad_out, log_sum_exp, key_cache, value_cache):
        row_delta = jnp.sum(grad_out.astype(F32) * attn_out.astype(F32), axis=-1)
        stats = jnp.stack([log_sum_exp * (-1.0 / SCALE), -row_delta], axis=0)
        stats = stats.reshape(2, N_GRP, 8, ROWS_DEV, N_DEV, GROUP)
        stats = jnp.transpose(stats, (4, 1, 0, 2, 3, 5)).reshape(N_DEV, N_GRP, 16, DIM)
        keys = jnp.transpose(key_cache, (1, 0, 2))
        values = jnp.transpose(value_cache, (1, 0, 2))
        dma = pltpu.SemaphoreType.DMA
        rows_shape = (N_DEV, N_GRP, 8, ROWS_DEV, GROUP, DIM)
        n_rg = N_DEV * N_GRP
        grad_query, grad_key, grad_value = pl.pallas_call(
            kernel,
            name='attn_bwd',
            out_shape=(jax.ShapeDtypeStruct((N_SLICES, ROWS_DEV, N_DEV * GROUP, DIM), BF16),
                       jax.ShapeDtypeStruct((N_DEV, KEYS_DEV, DIM), F32),
                       jax.ShapeDtypeStruct((N_DEV, KEYS_DEV, DIM), F32)),
            in_specs=[any_] * 5,
            out_specs=[any_] * 3,
            scratch_shapes=[
                pltpu.VMEM(rows_shape, BF16), pltpu.VMEM(rows_shape, BF16),
                pltpu.VMEM((n_rg, DIM, RB), BF16), pltpu.VMEM((n_rg, DIM, RB), BF16),
                pltpu.VMEM((N_DEV, N_GRP, 16, DIM), F32), pltpu.VMEM((N_DEV, N_GRP, DIM, DIM), BF16),
                pltpu.VMEM((KEYS, DIM), BF16), pltpu.VMEM((KEYS, DIM), BF16),
                pltpu.VMEM((n_rg, DIM, RB), F32),
                pltpu.VMEM((NKB, DIM, CB), F32), pltpu.VMEM((NKB, DIM, CB), F32),
                pltpu.VMEM((RB, CB), BF16), pltpu.VMEM((RB, CB), BF16),
                pltpu.VMEM((RB, CB), BF16), pltpu.VMEM((RB, CB), BF16),
                pltpu.VMEM((DIM, CB), jnp.int32),
                pltpu.VMEM((N_BUF, 2, CB, DIM), F32),
                pltpu.VMEM((2, N_GRP, 8, ROWS_DEV, GROUP, DIM), BF16),
                dma((N_DEV, N_GRP, 3)), dma((N_DEV, 2)), dma((N_DEV, N_GRP, 3)), dma((N_DEV, 2)),
                dma((N_BUF, 2)), dma((N_DEV, 2)), dma((2, N_GRP)), dma((N_DEV,)),
            ],
            compiler_params=pltpu.CompilerParams(collective_id=0, has_side_effects=True, vmem_limit_bytes=67043328),
        )(queries, grad_out, stats, keys, values)
        return grad_query, jnp.transpose(grad_key, (1, 0, 2)), jnp.transpose(grad_value, (1, 0, 2))

    return jax.shard_map(local_grads, mesh=mesh, in_specs=(row_spec, row_spec, row_spec, stat_spec, key_spec, key_spec),
                         out_specs=(row_spec, key_spec, key_spec), check_vma=False)
```

time: 663 us -> 555 us (0.84)
  Pallas kernels: 603 us -> 508 us
  local copies, waits for them, and re-layouts: 44.4 us -> 27.4 us
    pallas_call x1, Pallas kernels: 603 us -> 508 us  [local_grads(): pl.pallas_call(kernel, name='attn_bwd', out_shape=(jax.ShapeDtypeStruct((...]
    reshape x1, local copies, waits for them, and re-layouts: 7.92 us -> 1.1 us  [local_grads(): jnp.transpose(stats, (4, 1, 0, 2, 3, 5)).reshape(N_DEV, N_GRP, 16, DIM)]
    unnamed x26 -> x11, local copies, waits for them, and re-layouts: 25.8 us -> 19.9 us
where the time goes in v2:
time: 555 us; the launch traced here: 544 us
  Pallas kernels  508 us (92%)
  local copies, waits for them, and re-layouts  27.4 us (5%)
  other arithmetic  8.16 us (1%)
    pallas_call x1, Pallas kernels, local_grads(): pl.pallas_call(kernel, name='attn_bwd', out_shape=(jax.ShapeDtypeStruct((...  508 us
    unnamed x11, local copies, waits for them, and re-layouts  19.9 us

profile of v2, /device:TPU:0, one launch (start us, length us, event | category | flops | bytes accessed | tf_op | source)
XLA Modules:
  0.0 544.2 jit_solution(9659164332912064116)
XLA Ops:
  0.6 0.0 copy-start.1
  0.6 7.9 %multiply_reduce_fusion = f32[24,8,128]{2,1,0:T(8,128)S(1)} fusion(bf16[24,8,128,128]{3,2,1,0:T(8,128)(2,1)} %param.7, bf16[24,8,128,128]{3,2,1,0:T(8,128)(2,1)} %do_h.1), kind=kLoop, calls=%fused_computation | loop fusion | flops 12558336 | bytes 12681216 | tf_op jit(solution)/shard_map/reduce_sum | solution.py:463
  8.6 0.0 copy-done.1
  8.6 0.2 stack.7
  8.9 0.2 neg.15
  9.1 0.2 maximum_bitcast_fusion
  9.3 0.3 copy.14
  9.7 1.1 reshape.25.st_h
  10.8 5.6 %copy_bitcast_fusion = (bf16[8,1216,128]{2,1,0:T(8,128)(2,1)}, bf16[8,1216,128]{2,1,0:T(8,128)(2,1)}) fusion(bf16[1216,8,128]{2,1,0:T(8,128)(2,1)} %param.11, bf16[1216,8,128]{2,1,0:T(8,128)(2,1)} %param.10), kind=kLoop, calls=%fused_computation.1 | loop fusion | bytes 9961472 | tf_op jit(solution)/shard_map/transpose | solution.py:468
  16.4 507.9 %attn_bwd.1 = (bf16[24,8,128,128]{3,2,1,0:T(8,128)(2,1)}, f32[8,1216,128]{2,1,0:T(8,128)}, f32[8,1216,128]{2,1,0:T(8,128)}) custom-call(bf16[24,8,128,128]{3,2,1,0:T(8,128)(2,1)} %q_h.1, bf16[24,8,128,128]{3,2,1,0:T(8,128)(2,1)} %do_h.1, f32[8,3,16,128]{3,2,1,0:T(8,128)} %reshape.25.st_h, bf16[8,1216,128]{2,1,0:T(8,128)(2,1)} %get-tuple-element.16.k_h, ...), custom_call_target="tpu_custom_call" | custom-call | tf_op jit(solution)/shard_map/attn_bwd/pallas_call | solution.py:472
  524.3 0.0 copy-start
  524.3 0.0 slice-start
  524.3 9.3 %copy.17 = f32[1216,8,128]{2,1,0:T(8,128)} copy(f32[1216,8,128]{2,0,1:T(8,128)} %bitcast.13) | data formatting | bytes 9961472
  533.6 0.0 copy-done
  533.6 0.0 slice-start.1
  533.6 7.9 %copy.18 = f32[1216,8,128]{2,1,0:T(8,128)} copy(f32[1216,8,128]{2,0,1:T(8,128)S(1)} %bitcast.12) | data formatting | bytes 9961472
  541.5 0.0 slice-done
  541.5 0.0 slice-done.1
  541.5 2.7 copy.22
  (3 shorter events, 0.0 us)
Async XLA Ops:
  0.6 8.0 %copy-start.1 = (f32[24,8,128]{2,1,0:T(8,128)S(1)}, f32[24,8,128]{2,1,0:T(8,128)}, u32[]{:S(2)}) copy-start(f32[24,8,128]{2,1,0:T(8,128)} %param.9) | copy-start | bytes 294916
  524.3 9.3 %copy-start = (f32[8,1216,128]{2,1,0:T(8,128)S(1)}, f32[8,1216,128]{2,1,0:T(8,128)}, u32[]{:S(2)}) copy-start(f32[8,1216,128]{2,1,0:T(8,128)} %get-tuple-element.8) | copy-start | bytes 14942212
  524.3 17.2 %slice-start = ((s8[6291456]{0:T(1024)(128)(4,1)}), s8[4194304]{0:T(1024)(128)(4,1)S(1)}, s32[]{:S(2)}) async-start(s8[6291456]{0:T(1024)(128)(4,1)} %bitcast.10), calls=%async_computation | async-start | bytes 8388608
  533.6 7.9 %slice-start.1 = ((s8[6291456]{0:T(1024)(128)(4,1)}), s8[2097152]{0:T(1024)(128)(4,1)S(1)}, s32[]{:S(2)}) async-start(s8[6291456]{0:T(1024)(128)(4,1)} %bitcast.10), calls=%async_computation.1 | async-start | bytes 4194304
